TPU v7x, 32 devices: a whole 2x2x4 slice. The times are simulated.
32 devices in a mesh: dp: 8 (over z, y), mp: 4 (over x, core).
Axes of the slice: x: 2, y: 2, z: 4, core: 2. Of those that a mesh axis runs over, the one named last changes fastest.
Arguments:
- slow_weights: float32 [1, 3584, 1024], P(None, None, 'mp'), may hold values from -6 to 6
- fast_weights: bfloat16 [8, 1, 3584, 1024], P('dp', None, None, 'mp'), may hold values from -64 to 64
- momentum: float32 [1, 3584, 1024], P(None, None, 'mp'), may hold values from -1.2 to 1.2
Outputs:
- slow_next: float32 [1, 3584, 1024], P(None, None, 'mp')
- momentum_next: float32 [1, 3584, 1024], P(None, None, 'mp')
- fast_next: bfloat16 [8, 1, 3584, 1024], P('dp', None, None, 'mp')
All inputs are finite; a program needn't handle non-finite values.
Results may differ from a plain program's by a relative error of at most 0.001.
Values sent between devices are 32-bit elements; how exact they have to be, the bound alone decides.
No kernel may reach another device: no remote copies, remote signals or barrier semaphores. Data moves between devices by JAX's collectives and lax.ppermute only.
A program may use at most 64 MiB of HBM per device.

v0:
```python
import functools
import math

import jax
import jax.numpy as jnp
from jax import lax
from jax.experimental import pallas as pl
from jax.experimental.pallas import tpu as pltpu
from jax.sharding import PartitionSpec as P


MOMENTUM_RATE = 0.9
OUTER_RATE = 0.7
CLIP_LEVEL = 0.2
EPSILON = 1e-06
STREAMS = 4
GAP = 4
LATE = 2
VMEM = pl.BlockSpec(memory_space=pltpu.VMEM)
SMEM = pl.BlockSpec(memory_space=pltpu.SMEM)
HBM = pl.BlockSpec(memory_space=pltpu.HBM)


def split(rows, tile=8):
    tiles = rows // tile
    edges = [tile * (tiles * s // STREAMS) for s in range(STREAMS)] + [rows]
    return [(a, b - a) for a, b in zip(edges[:-1], edges[1:])]


def chunk_index(n, back):
    me = lax.axis_index("dp")
    way = 2 * lax.rem(lax.axis_index("mp"), 2) - 1
    if n % 2:
        place = me
    else:
        half = lax.div(me, 2)
        place = jnp.where(lax.rem(me, 2) == 0, half, n - 1 - half)
    return lax.rem(place + way * back + 2 * n, n)


def estimate(elements, bytes_each, flops_each):
    return pl.CostEstimate(
        flops=flops_each * elements, bytes_accessed=bytes_each * elements, transcendentals=0
    )


def grant(byte_count):
    return pltpu.CompilerParams(vmem_limit_bytes=byte_count + (1 << 20))


def first_kernel(n, start, rows, slow_ref, fast_ref, out_ref, slow_buf, fast_buf, sems):
    here = (chunk_index(n, 1), pl.ds(start, rows))
    a = pltpu.make_async_copy(slow_ref.at[here], slow_buf, sems.at[0])
    b = pltpu.make_async_copy(fast_ref.at[here], fast_buf, sems.at[1])
    a.start()
    b.start()
    a.wait()
    b.wait()
    out_ref[...] = slow_buf[...] - fast_buf[...].astype(jnp.float32)


def first_piece(slow, fast, n, part):
    columns = slow.shape[2]
    rows = part[1]
    slow = pltpu.with_memory_space_constraint(slow, pltpu.HBM)
    fast = pltpu.with_memory_space_constraint(fast, pltpu.HBM)
    return pl.pallas_call(
        functools.partial(first_kernel, n, *part),
        out_shape=jax.ShapeDtypeStruct((rows, columns), jnp.float32),
        in_specs=[HBM, HBM],
        out_specs=VMEM,
        scratch_shapes=[
            pltpu.VMEM((rows, columns), jnp.float32),
            pltpu.VMEM((rows, columns), jnp.bfloat16),
            pltpu.SemaphoreType.DMA((2,)),
        ],
        cost_estimate=estimate(rows * columns, 10, 1),
        compiler_params=grant(rows * columns * 6),
        name="first",
    )(slow, fast)


def own_kernel(n, start, rows, slow_ref, fast_ref, out_ref):
    here = (chunk_index(n, 1), pl.ds(start, rows))
    out_ref[...] = slow_ref[here] - fast_ref[here].astype(jnp.float32)


def own_piece(slow, fast, n, part):
    shape = (part[1], slow.shape[2])
    return pl.pallas_call(
        functools.partial(own_kernel, n, *part),
        out_shape=jax.ShapeDtypeStruct(shape, jnp.float32),
        in_specs=[VMEM, VMEM],
        out_specs=VMEM,
        cost_estimate=estimate(shape[0] * shape[1], 10, 1),
        compiler_params=grant(0),
        name="own",
    )(slow, fast)


def add_kernel(n, back, start, rows, got_ref, slow_ref, fast_ref, *refs):
    here = (chunk_index(n, back), pl.ds(start, rows))
    refs[-1][...] = got_ref[...] + (slow_ref[here] - fast_ref[here].astype(jnp.float32))


def add_piece(got, state, n, back, part):
    return pl.pallas_call(
        functools.partial(add_kernel, n, back, *part),
        out_shape=jax.ShapeDtypeStruct(got.shape, jnp.float32),
        in_specs=[VMEM] * (1 + len(state)),
        out_specs=VMEM,
        cost_estimate=estimate(got.size, 160, 2),
        compiler_params=grant(0),
        name="add",
    )(got, *state)


def tally_kernel(n, chunks, *refs):
    out = refs[-1]
    place = lax.broadcasted_iota(jnp.int32, out.shape, 0)
    table = jnp.zeros(out.shape, jnp.float32)
    for back, positions in chunks:
        squares = jnp.zeros((8, 128), jnp.float32)
        for k in positions:
            mean = refs[k][...] * (1.0 / n)
            squares = squares + jnp.sum((mean * mean).reshape(-1, 8, 128), axis=0)
        row = jnp.sum(squares, axis=0, keepdims=True)
        table = jnp.where(place == chunk_index(n, back), row, table)
    out[...] = table


def tally(chunks, state, n):
    pieces = [piece for chunk in chunks for piece in chunk]
    count = len(chunks[0])
    spans = [(chunk[0][0], range(count * k, count * (k + 1))) for k, chunk in enumerate(chunks)]
    values = [sums for _, _, sums in pieces]
    return pl.pallas_call(
        functools.partial(tally_kernel, n, spans),
        out_shape=jax.ShapeDtypeStruct((-(-n // 8) * 8, 128), jnp.float32),
        in_specs=[VMEM] * (len(values) + len(state)),
        out_specs=VMEM,
        cost_estimate=estimate(sum(v.size for v in values), 40, 3),
        compiler_params=grant(0),
        name="tally",
    )(*values, *state)


def sum_kernel(*refs):
    refs[-1][...] = refs[0][...] + refs[1][...]


def sum_small(a, b, state):
    return pl.pallas_call(
        sum_kernel,
        out_shape=jax.ShapeDtypeStruct(a.shape, jnp.float32),
        in_specs=[VMEM] * (2 + len(state)),
        out_specs=VMEM,
        cost_estimate=estimate(a.size, 12, 1),
        compiler_params=grant(0),
        name="sum",
    )(a, b, *state)


def update_kernel(n, max_norm, pieces, n_outs, total_ref, slow_ref, momentum_ref, *refs):
    count = len(pieces)
    sums = refs[:count]
    slow_out, momentum_out, fast_out = refs[count + n_outs : count + n_outs + 3]
    slow_buf, momentum_buf, fast_buf, sems = refs[count + n_outs + 3 :]
    norm = jnp.sqrt(jnp.sum(total_ref[...], keepdims=True))
    factor = jnp.minimum(1.0, max_norm / (norm + EPSILON))
    copies = []
    at = 0
    for k, (back, start, rows) in enumerate(pieces):
        index = chunk_index(n, back)
        here, there = pl.ds(start, rows), pl.ds(at, rows)
        gradient = factor * (sums[k][...] * (1.0 / n))
        momentum_next = MOMENTUM_RATE * momentum_ref[index, here] + gradient
        slow_next = slow_ref[index, here] - OUTER_RATE * (gradient + MOMENTUM_RATE * momentum_next)
        slow_buf[there] = slow_next
        momentum_buf[there] = momentum_next
        fast_buf[there] = slow_next.astype(jnp.bfloat16)
        for j, (buf, out) in enumerate(
            ((slow_buf, slow_out), (momentum_buf, momentum_out), (fast_buf, fast_out))
        ):
            copy = pltpu.make_async_copy(buf.at[there], out.at[index, here], sems.at[j, k])
            copy.start()
            copies.append(copy)
        at += rows
    for copy in copies:
        copy.wait()


def update(total, chunks, slow, momentum, outs, n, max_norm):
    pieces = [(back, start, rows) for back, (start, rows), _ in chunks]
    count = len(chunks)
    columns = slow.shape[2]
    rows = sum(rows for _, _, rows in pieces)
    return pl.pallas_call(
        functools.partial(update_kernel, n, max_norm, pieces, len(outs)),
        out_shape=(
            pltpu.HBM(slow.shape, jnp.float32),
            pltpu.HBM(slow.shape, jnp.float32),
            pltpu.HBM(slow.shape, jnp.bfloat16),
        ),
        in_specs=[VMEM, VMEM, VMEM] + [VMEM] * count + [HBM] * len(outs),
        out_specs=(HBM, HBM, HBM),
        scratch_shapes=[
            pltpu.VMEM((rows, columns), jnp.float32),
            pltpu.VMEM((rows, columns), jnp.float32),
            pltpu.VMEM((rows, columns), jnp.bfloat16),
            pltpu.SemaphoreType.DMA((3, count)),
        ],
        input_output_aliases={3 + count + k: k for k in range(len(outs))},
        cost_estimate=estimate(rows * columns, 22, 8),
        compiler_params=grant(rows * columns * 15),
        name="update",
    )(total, slow, momentum, *[sums for _, _, sums in chunks], *outs)


def ring_order(n):
    if n % 2:
        return list(range(n))
    return [2 * k for k in range(n // 2)] + [n - 1 - 2 * k for k in range(n // 2)]


def ring_perm(n, m):
    order = ring_order(n)
    perm = []
    for k in range(n):
        for c in range(m):
            other = (k + 1) % n if c % 2 == 0 else (k - 1) % n
            perm.append((order[k] * m + c, order[other] * m + c))
    return perm


def exchanges(n, m):
    order = ring_order(n)
    across = None if n % 2 else [(order[k], order[(k + n // 2) % n]) for k in range(n)]
    steps = [("dp", across)]
    if m & (m - 1):
        return steps + [("mp", None)]
    bit = 1
    while bit < m:
        steps.append(("mp", [(i, i ^ bit) for i in range(m)]))
        bit *= 2
    return steps


def exchange_slots(n, m):
    count = len(exchanges(n, m))
    return [STREAMS * (n - 1) - GAP * (count - j) for j in range(count)]


def body(slow_weights, fast_weights, momentum):
    n, m = lax.axis_size("dp"), lax.axis_size("mp")
    rows, columns = slow_weights.shape[1:]
    max_norm = CLIP_LEVEL * math.sqrt(slow_weights.size * m)
    depth = rows // n
    slow = slow_weights.reshape(n, depth, columns)
    fast = fast_weights.reshape(n, depth, columns)
    moment = momentum.reshape(n, depth, columns)
    parts = split(depth)
    perm = ring_perm(n, m)
    steps, slots = exchanges(n, m), exchange_slots(n, m)

    def hop(value):
        return lax.ppermute(value, ("dp", "mp"), perm)

    held = [first_piece(slow, fast, n, parts[0])]
    held += [own_piece(slow, fast, n, part) for part in parts[1:]]
    for step in range(n - 1):
        state = (slow, fast) if step < LATE else (slow, fast, moment)
        for s, part in enumerate(parts):
            held[s] = add_piece(hop(held[s]), state, n, step + 2, part)

    state = (slow, moment)
    chunks = [[(0, part, held[s]) for s, part in enumerate(parts)]]
    table, arriving = None, None
    for slot in range(STREAMS * (n - 1)):
        step, s = divmod(slot, STREAMS)
        if slot in slots:
            j = slots.index(slot)
            if j == 0:
                known = 1 if n % 2 else n // 2
                table = tally(chunks[:known], state, n)
            else:
                table = sum_small(table, arriving, state)
            axis, pairs = steps[j]
            if pairs is None:
                arriving = lax.psum(table, axis) - table
            else:
                arriving = lax.ppermute(table, axis, pairs)
        held[s] = hop(held[s])
        if s == 0:
            chunks.append([])
        chunks[-1].append((step + 1, parts[s], held[s]))
    table = sum_small(table, arriving, state)

    mine = [piece for chunk in chunks[:-1] for piece in chunk]
    outs = update(table, mine, slow, moment, (), n, max_norm)
    outs = update(table, chunks[-1], slow, moment, outs, n, max_norm)
    slow_next, momentum_next, fast_next = outs
    return (
        slow_next.reshape(slow_weights.shape),
        momentum_next.reshape(momentum.shape),
        fast_next.reshape(fast_weights.shape),
    )


def solution(mesh):
    in_specs = (P(None, None, "mp"), P("dp", None, None, "mp"), P(None, None, "mp"))
    out_specs = (P(None, None, "mp"), P(None, None, "mp"), P("dp", None, None, "mp"))
    return jax.shard_map(body, mesh=mesh, in_specs=in_specs, out_specs=out_specs, check_vma=False)
```

profile of v0, /device:TPU:0, one launch (start us, length us, event | category | flops | bytes accessed | tf_op | source)
XLA Modules:
  0.0 90.7 jit_solution(6294139026929096953)
XLA Ops:
  1.8 3.1 %collective-permute-start = (f32[112,256]{1,0:T(8,128)S(1)}, f32[112,256]{1,0:T(8,128)S(1)}, u32[]{:S(2)}, u32[]{:S(2)}) collective-permute-start(f32[112,256]{1,0:T(8,128)S(1)} %first.1), channel_id=1, source_target_pairs={{0,8},{1,5},{2,10},{3,7},{8,16},{9,1},{10,18},{11,3},{16,24},{17,9... | collective-permute-start | bytes 344072 | tf_op jit(solution)/shard_map/ppermute | solution.py:267
  4.9 1.6 %collective-permute-start.7 = (f32[112,256]{1,0:T(8,128)S(1)}, f32[112,256]{1,0:T(8,128)S(1)}, u32[]{:S(2)}, u32[]{:S(2)}) collective-permute-start(f32[112,256]{1,0:T(8,128)S(1)} %own.3), channel_id=1, source_target_pairs={{0,8},{1,5},{2,10},{3,7},{8,16},{9,1},{10,18},{11,3},{16,24},{17,9... | collective-permute-start | bytes 344072 | tf_op jit(solution)/shard_map/ppermute | solution.py:267
  6.5 1.6 %collective-permute-start.14 = (f32[112,256]{1,0:T(8,128)S(1)}, f32[112,256]{1,0:T(8,128)S(1)}, u32[]{:S(2)}, u32[]{:S(2)}) collective-permute-start(f32[112,256]{1,0:T(8,128)S(1)} %own.4), channel_id=1, source_target_pairs={{0,8},{1,5},{2,10},{3,7},{8,16},{9,1},{10,18},{11,3},{16,24},{17,9... | collective-permute-start | bytes 344072 | tf_op jit(solution)/shard_map/ppermute | solution.py:267
  8.2 1.6 %collective-permute-start.21 = (f32[112,256]{1,0:T(8,128)S(1)}, f32[112,256]{1,0:T(8,128)S(1)}, u32[]{:S(2)}, u32[]{:S(2)}) collective-permute-start(f32[112,256]{1,0:T(8,128)S(1)} %own.5), channel_id=1, source_target_pairs={{0,8},{1,5},{2,10},{3,7},{8,16},{9,1},{10,18},{11,3},{16,24},{17,9... | collective-permute-start | bytes 344072 | tf_op jit(solution)/shard_map/ppermute | solution.py:267
  9.8 1.5 %collective-permute-start.1 = (f32[112,256]{1,0:T(8,128)S(1)}, f32[112,256]{1,0:T(8,128)S(1)}, u32[]{:S(2)}, u32[]{:S(2)}) collective-permute-start(f32[112,256]{1,0:T(8,128)S(1)} %add.28), channel_id=1, source_target_pairs={{0,8},{1,5},{2,10},{3,7},{8,16},{9,1},{10,18},{11,3},{16,24},{17,9... | collective-permute-start | bytes 344072 | tf_op jit(solution)/shard_map/ppermute | solution.py:267
  13.1 1.6 %collective-permute-start.22 = (f32[112,256]{1,0:T(8,128)S(1)}, f32[112,256]{1,0:T(8,128)S(1)}, u32[]{:S(2)}, u32[]{:S(2)}) collective-permute-start(f32[112,256]{1,0:T(8,128)S(1)} %add.49), channel_id=1, source_target_pairs={{0,8},{1,5},{2,10},{3,7},{8,16},{9,1},{10,18},{11,3},{16,24},{17,9... | collective-permute-start | bytes 344072 | tf_op jit(solution)/shard_map/ppermute | solution.py:267
  14.7 1.5 %collective-permute-start.2 = (f32[112,256]{1,0:T(8,128)S(1)}, f32[112,256]{1,0:T(8,128)S(1)}, u32[]{:S(2)}, u32[]{:S(2)}) collective-permute-start(f32[112,256]{1,0:T(8,128)S(1)} %add.29), channel_id=1, source_target_pairs={{0,8},{1,5},{2,10},{3,7},{8,16},{9,1},{10,18},{11,3},{16,24},{17,9... | collective-permute-start | bytes 344072 | tf_op jit(solution)/shard_map/ppermute | solution.py:267
  16.2 1.2 %collective-permute-start.9 = (f32[112,256]{1,0:T(8,128)S(1)}, f32[112,256]{1,0:T(8,128)S(1)}, u32[]{:S(2)}, u32[]{:S(2)}) collective-permute-start(f32[112,256]{1,0:T(8,128)S(1)} %add.36), channel_id=1, source_target_pairs={{0,8},{1,5},{2,10},{3,7},{8,16},{9,1},{10,18},{11,3},{16,24},{17,9... | collective-permute-start | bytes 344072 | tf_op jit(solution)/shard_map/ppermute | solution.py:267
  18.7 1.2 %collective-permute-start.23 = (f32[112,256]{1,0:T(8,128)S(1)}, f32[112,256]{1,0:T(8,128)S(1)}, u32[]{:S(2)}, u32[]{:S(2)}) collective-permute-start(f32[112,256]{1,0:T(8,128)S(1)} %add.50), channel_id=1, source_target_pairs={{0,8},{1,5},{2,10},{3,7},{8,16},{9,1},{10,18},{11,3},{16,24},{17,9... | collective-permute-start | bytes 344072 | tf_op jit(solution)/shard_map/ppermute | solution.py:267
  21.2 1.2 %collective-permute-start.10 = (f32[112,256]{1,0:T(8,128)S(1)}, f32[112,256]{1,0:T(8,128)S(1)}, u32[]{:S(2)}, u32[]{:S(2)}) collective-permute-start(f32[112,256]{1,0:T(8,128)S(1)} %add.37), channel_id=1, source_target_pairs={{0,8},{1,5},{2,10},{3,7},{8,16},{9,1},{10,18},{11,3},{16,24},{17,9... | collective-permute-start | bytes 344072 | tf_op jit(solution)/shard_map/ppermute | solution.py:267
  26.1 1.2 %collective-permute-start.11 = (f32[112,256]{1,0:T(8,128)S(1)}, f32[112,256]{1,0:T(8,128)S(1)}, u32[]{:S(2)}, u32[]{:S(2)}) collective-permute-start(f32[112,256]{1,0:T(8,128)S(1)} %add.38), channel_id=1, source_target_pairs={{0,8},{1,5},{2,10},{3,7},{8,16},{9,1},{10,18},{11,3},{16,24},{17,9... | collective-permute-start | bytes 344072 | tf_op jit(solution)/shard_map/ppermute | solution.py:267
  28.5 1.2 %collective-permute-start.25 = (f32[112,256]{1,0:T(8,128)S(1)}, f32[112,256]{1,0:T(8,128)S(1)}, u32[]{:S(2)}, u32[]{:S(2)}) collective-permute-start(f32[112,256]{1,0:T(8,128)S(1)} %add.52), channel_id=1, source_target_pairs={{0,8},{1,5},{2,10},{3,7},{8,16},{9,1},{10,18},{11,3},{16,24},{17,9... | collective-permute-start | bytes 344072 | tf_op jit(solution)/shard_map/ppermute | solution.py:267
  31.0 1.2 %collective-permute-start.12 = (f32[112,256]{1,0:T(8,128)S(1)}, f32[112,256]{1,0:T(8,128)S(1)}, u32[]{:S(2)}, u32[]{:S(2)}) collective-permute-start(f32[112,256]{1,0:T(8,128)S(1)} %add.39), channel_id=1, source_target_pairs={{0,8},{1,5},{2,10},{3,7},{8,16},{9,1},{10,18},{11,3},{16,24},{17,9... | collective-permute-start | bytes 344072 | tf_op jit(solution)/shard_map/ppermute | solution.py:267
  33.4 1.2 %collective-permute-start.26 = (f32[112,256]{1,0:T(8,128)S(1)}, f32[112,256]{1,0:T(8,128)S(1)}, u32[]{:S(2)}, u32[]{:S(2)}) collective-permute-start(f32[112,256]{1,0:T(8,128)S(1)} %add.53), channel_id=1, source_target_pairs={{0,8},{1,5},{2,10},{3,7},{8,16},{9,1},{10,18},{11,3},{16,24},{17,9... | collective-permute-start | bytes 344072 | tf_op jit(solution)/shard_map/ppermute | solution.py:267
  35.9 1.2 %collective-permute-start.13 = (f32[112,256]{1,0:T(8,128)S(1)}, f32[112,256]{1,0:T(8,128)S(1)}, u32[]{:S(2)}, u32[]{:S(2)}) collective-permute-start(f32[112,256]{1,0:T(8,128)S(1)} %add.40), channel_id=1, source_target_pairs={{0,8},{1,5},{2,10},{3,7},{8,16},{9,1},{10,18},{11,3},{16,24},{17,9... | collective-permute-start | bytes 344072 | tf_op jit(solution)/shard_map/ppermute | solution.py:267
  38.4 1.2 %collective-permute-start.27 = (f32[112,256]{1,0:T(8,128)S(1)}, f32[112,256]{1,0:T(8,128)S(1)}, u32[]{:S(2)}, u32[]{:S(2)}) collective-permute-start(f32[112,256]{1,0:T(8,128)S(1)} %add.54), channel_id=1, source_target_pairs={{0,8},{1,5},{2,10},{3,7},{8,16},{9,1},{10,18},{11,3},{16,24},{17,9... | collective-permute-start | bytes 344072 | tf_op jit(solution)/shard_map/ppermute | solution.py:267
  40.8 1.2 %collective-permute-start.29 = (f32[112,256]{1,0:T(8,128)S(1)}, f32[112,256]{1,0:T(8,128)S(1)}, u32[]{:S(2)}, u32[]{:S(2)}) collective-permute-start(f32[112,256]{1,0:T(8,128)S(1)} %add.41.refs_1_), channel_id=1, source_target_pairs={{0,8},{1,5},{2,10},{3,7},{8,16},{9,1},{10,18},{11,3},{16,24},{17,9... | collective-permute-start | bytes 344072 | tf_op jit(solution)/shard_map/ppermute | solution.py:267
  43.3 1.2 %collective-permute-start.31 = (f32[112,256]{1,0:T(8,128)S(1)}, f32[112,256]{1,0:T(8,128)S(1)}, u32[]{:S(2)}, u32[]{:S(2)}) collective-permute-start(f32[112,256]{1,0:T(8,128)S(1)} %add.55.refs_3_), channel_id=1, source_target_pairs={{0,8},{1,5},{2,10},{3,7},{8,16},{9,1},{10,18},{11,3},{16,24},{17,9... | collective-permute-start | bytes 344072 | tf_op jit(solution)/shard_map/ppermute | solution.py:267
  74.2 2.3 %collective-permute-start.40 = (f32[8,128]{1,0:T(8,128)S(1)}, f32[8,128]{1,0:T(8,128)S(1)}, u32[]{:S(2)}, u32[]{:S(2)}) collective-permute-start(f32[8,128]{1,0:T(8,128)S(1)} %tally.1.refs_0_), channel_id=1, source_target_pairs={{0,28},{8,20},{16,12},{24,4},{28,0},{20,8},{12,16},{4,24},{1,29},{... | collective-permute-start | bytes 12296 | tf_op jit(solution)/shard_map/ppermute | solution.py:292
  76.5 4.1 %collective-permute-done.40.refs_1_ = f32[8,128]{1,0:T(8,128)S(1)} collective-permute-done((f32[8,128]{1,0:T(8,128)S(1)}, f32[8,128]{1,0:T(8,128)S(1)}, u32[]{:S(2)}, u32[]{:S(2)}) %collective-permute-start.40) | collective-permute-done | bytes 4128 | tf_op jit(solution)/shard_map/ppermute | solution.py:292
  81.7 1.5 %collective-permute-start.42 = (f32[8,128]{1,0:T(8,128)S(1)}, f32[8,128]{1,0:T(8,128)S(1)}, u32[]{:S(2)}, u32[]{:S(2)}) collective-permute-start(f32[8,128]{1,0:T(8,128)S(1)} %sum.4.refs_0_), channel_id=1, source_target_pairs={{0,2},{1,3},{2,0},{3,1},{4,6},{5,7},{6,4},{7,5},{8,10},{9,11},{10,... | collective-permute-start | bytes 12296 | tf_op jit(solution)/shard_map/ppermute | solution.py:292
  83.2 2.1 %collective-permute-done.42.refs_1_ = f32[8,128]{1,0:T(8,128)S(1)} collective-permute-done((f32[8,128]{1,0:T(8,128)S(1)}, f32[8,128]{1,0:T(8,128)S(1)}, u32[]{:S(2)}, u32[]{:S(2)}) %collective-permute-start.42) | collective-permute-done | bytes 4128 | tf_op jit(solution)/shard_map/ppermute | solution.py:292
  85.3 4.0 %update.2 = (f32[8,448,256]{2,1,0:T(8,128)}, f32[8,448,256]{2,1,0:T(8,128)}, bf16[8,448,256]{2,1,0:T(8,128)(2,1)}) custom-call(f32[8,128]{1,0:T(8,128)S(1)} %sum.5.total_ref, f32[8,448,256]{2,1,0:T(8,128)S(1)} %bitcast.42, f32[8,448,256]{2,1,0:T(8,128)S(1)} %bitcast.68, f32[112,256]{1,0:T(8,128)S(1)} %add.34.refs_0_, f32[112,256]{1,0:T(8,128)S(1)} %add.41.refs_1_, ...), custom_call_target="tpu_custom_call" | custom-call | flops 6422528 | bytes 17661952 | tf_op jit(solution)/shard_map/update/pallas_call | solution.py:198
  89.4 1.3 %update.3 = (f32[8,448,256]{2,1,0:T(8,128)}, f32[8,448,256]{2,1,0:T(8,128)}, bf16[8,448,256]{2,1,0:T(8,128)(2,1)}) custom-call(f32[8,128]{1,0:T(8,128)S(1)} %sum.5.total_ref, f32[8,448,256]{2,1,0:T(8,128)S(1)} %bitcast.43, f32[8,448,256]{2,1,0:T(8,128)S(1)} %bitcast.69, ...), custom_call_target="tpu_custom_call", output_to_operand_aliasing={{0}: (7, {}), {1}: (8, {}), {2}: (9, {})} | custom-call | flops 917504 | bytes 2523136 | tf_op jit(solution)/shard_map/update/pallas_call | solution.py:198
  (138 shorter events, 48.7 us)
Async XLA Ops:
  1.8 8.0 %collective-permute-start = (f32[112,256]{1,0:T(8,128)S(1)}, f32[112,256]{1,0:T(8,128)S(1)}, u32[]{:S(2)}, u32[]{:S(2)}) collective-permute-start(f32[112,256]{1,0:T(8,128)S(1)} %first.1), channel_id=1, source_target_pairs={{0,8},{1,5},{2,10},{3,7},{8,16},{9,1},{10,18},{11,3},{16,24},{17,9... | collective-permute-start | bytes 344072 | tf_op jit(solution)/shard_map/ppermute | solution.py:267
  4.9 6.4 %collective-permute-start.7 = (f32[112,256]{1,0:T(8,128)S(1)}, f32[112,256]{1,0:T(8,128)S(1)}, u32[]{:S(2)}, u32[]{:S(2)}) collective-permute-start(f32[112,256]{1,0:T(8,128)S(1)} %own.3), channel_id=1, source_target_pairs={{0,8},{1,5},{2,10},{3,7},{8,16},{9,1},{10,18},{11,3},{16,24},{17,9... | collective-permute-start | bytes 344072 | tf_op jit(solution)/shard_map/ppermute | solution.py:267
  6.5 5.3 %collective-permute-start.14 = (f32[112,256]{1,0:T(8,128)S(1)}, f32[112,256]{1,0:T(8,128)S(1)}, u32[]{:S(2)}, u32[]{:S(2)}) collective-permute-start(f32[112,256]{1,0:T(8,128)S(1)} %own.4), channel_id=1, source_target_pairs={{0,8},{1,5},{2,10},{3,7},{8,16},{9,1},{10,18},{11,3},{16,24},{17,9... | collective-permute-start | bytes 344072 | tf_op jit(solution)/shard_map/ppermute | solution.py:267
  11.9 5.6 %collective-permute-start.15 = (f32[112,256]{1,0:T(8,128)S(1)}, f32[112,256]{1,0:T(8,128)S(1)}, u32[]{:S(2)}, u32[]{:S(2)}) collective-permute-start(f32[112,256]{1,0:T(8,128)S(1)} %add.42), channel_id=1, source_target_pairs={{0,8},{1,5},{2,10},{3,7},{8,16},{9,1},{10,18},{11,3},{16,24},{17,9... | collective-permute-start | bytes 344072 | tf_op jit(solution)/shard_map/ppermute | solution.py:267
  13.1 5.6 %collective-permute-start.22 = (f32[112,256]{1,0:T(8,128)S(1)}, f32[112,256]{1,0:T(8,128)S(1)}, u32[]{:S(2)}, u32[]{:S(2)}) collective-permute-start(f32[112,256]{1,0:T(8,128)S(1)} %add.49), channel_id=1, source_target_pairs={{0,8},{1,5},{2,10},{3,7},{8,16},{9,1},{10,18},{11,3},{16,24},{17,9... | collective-permute-start | bytes 344072 | tf_op jit(solution)/shard_map/ppermute | solution.py:267
  14.7 5.2 %collective-permute-start.2 = (f32[112,256]{1,0:T(8,128)S(1)}, f32[112,256]{1,0:T(8,128)S(1)}, u32[]{:S(2)}, u32[]{:S(2)}) collective-permute-start(f32[112,256]{1,0:T(8,128)S(1)} %add.29), channel_id=1, source_target_pairs={{0,8},{1,5},{2,10},{3,7},{8,16},{9,1},{10,18},{11,3},{16,24},{17,9... | collective-permute-start | bytes 344072 | tf_op jit(solution)/shard_map/ppermute | solution.py:267
  16.2 4.9 %collective-permute-start.9 = (f32[112,256]{1,0:T(8,128)S(1)}, f32[112,256]{1,0:T(8,128)S(1)}, u32[]{:S(2)}, u32[]{:S(2)}) collective-permute-start(f32[112,256]{1,0:T(8,128)S(1)} %add.36), channel_id=1, source_target_pairs={{0,8},{1,5},{2,10},{3,7},{8,16},{9,1},{10,18},{11,3},{16,24},{17,9... | collective-permute-start | bytes 344072 | tf_op jit(solution)/shard_map/ppermute | solution.py:267
  45.7 4.9 %collective-permute-start.33 = (f32[112,256]{1,0:T(8,128)S(1)}, f32[112,256]{1,0:T(8,128)S(1)}, u32[]{:S(2)}, u32[]{:S(2)}) collective-permute-start(f32[112,256]{1,0:T(8,128)S(1)} %collective-permute-done.29.refs_5_), channel_id=1, source_target_pairs={{0,8},{1,5},{2,10},{3,7},{8,16},{9,1},{10,18},{11,3},{16,24},{17,9... | collective-permute-start | bytes 344072 | tf_op jit(solution)/shard_map/ppermute | solution.py:267
  48.1 4.9 %collective-permute-start.35 = (f32[112,256]{1,0:T(8,128)S(1)}, f32[112,256]{1,0:T(8,128)S(1)}, u32[]{:S(2)}, u32[]{:S(2)}) collective-permute-start(f32[112,256]{1,0:T(8,128)S(1)} %collective-permute-done.31.refs_7_), channel_id=1, source_target_pairs={{0,8},{1,5},{2,10},{3,7},{8,16},{9,1},{10,18},{11,3},{16,24},{17,9... | collective-permute-start | bytes 344072 | tf_op jit(solution)/shard_map/ppermute | solution.py:267
  49.4 4.9 %collective-permute-start.36 = (f32[112,256]{1,0:T(8,128)S(1)}, f32[112,256]{1,0:T(8,128)S(1)}, u32[]{:S(2)}, u32[]{:S(2)}) collective-permute-start(f32[112,256]{1,0:T(8,128)S(1)} %collective-permute-done.32.refs_8_), channel_id=1, source_target_pairs={{0,8},{1,5},{2,10},{3,7},{8,16},{9,1},{10,18},{11,3},{16,24},{17,9... | collective-permute-start | bytes 344072 | tf_op jit(solution)/shard_map/ppermute | solution.py:267
  50.6 4.9 %collective-permute-start.37 = (f32[112,256]{1,0:T(8,128)S(1)}, f32[112,256]{1,0:T(8,128)S(1)}, u32[]{:S(2)}, u32[]{:S(2)}) collective-permute-start(f32[112,256]{1,0:T(8,128)S(1)} %collective-permute-done.33.refs_9_), channel_id=1, source_target_pairs={{0,8},{1,5},{2,10},{3,7},{8,16},{9,1},{10,18},{11,3},{16,24},{17,9... | collective-permute-start | bytes 344072 | tf_op jit(solution)/shard_map/ppermute | solution.py:267
  51.8 4.9 %collective-permute-start.38 = (f32[112,256]{1,0:T(8,128)S(1)}, f32[112,256]{1,0:T(8,128)S(1)}, u32[]{:S(2)}, u32[]{:S(2)}) collective-permute-start(f32[112,256]{1,0:T(8,128)S(1)} %collective-permute-done.34.refs_10_), channel_id=1, source_target_pairs={{0,8},{1,5},{2,10},{3,7},{8,16},{9,1},{10,18},{11,3},{16,24},{17,9... | collective-permute-start | bytes 344072 | tf_op jit(solution)/shard_map/ppermute | solution.py:267
  53.1 4.9 %collective-permute-start.39 = (f32[112,256]{1,0:T(8,128)S(1)}, f32[112,256]{1,0:T(8,128)S(1)}, u32[]{:S(2)}, u32[]{:S(2)}) collective-permute-start(f32[112,256]{1,0:T(8,128)S(1)} %collective-permute-done.35.refs_11_), channel_id=1, source_target_pairs={{0,8},{1,5},{2,10},{3,7},{8,16},{9,1},{10,18},{11,3},{16,24},{17,9... | collective-permute-start | bytes 344072 | tf_op jit(solution)/shard_map/ppermute | solution.py:267
  54.3 4.9 %collective-permute-start.43 = (f32[112,256]{1,0:T(8,128)S(1)}, f32[112,256]{1,0:T(8,128)S(1)}, u32[]{:S(2)}, u32[]{:S(2)}) collective-permute-start(f32[112,256]{1,0:T(8,128)S(1)} %collective-permute-done.36.refs_12_), channel_id=1, source_target_pairs={{0,8},{1,5},{2,10},{3,7},{8,16},{9,1},{10,18},{11,3},{16,24},{17,9... | collective-permute-start | bytes 344072 | tf_op jit(solution)/shard_map/ppermute | solution.py:267
  55.5 4.9 %collective-permute-start.47 = (f32[112,256]{1,0:T(8,128)S(1)}, f32[112,256]{1,0:T(8,128)S(1)}, u32[]{:S(2)}, u32[]{:S(2)}) collective-permute-start(f32[112,256]{1,0:T(8,128)S(1)} %collective-permute-done.37.refs_13_), channel_id=1, source_target_pairs={{0,8},{1,5},{2,10},{3,7},{8,16},{9,1},{10,18},{11,3},{16,24},{17,9... | collective-permute-start | bytes 344072 | tf_op jit(solution)/shard_map/ppermute | solution.py:267
  56.7 4.9 %collective-permute-start.51 = (f32[112,256]{1,0:T(8,128)S(1)}, f32[112,256]{1,0:T(8,128)S(1)}, u32[]{:S(2)}, u32[]{:S(2)}) collective-permute-start(f32[112,256]{1,0:T(8,128)S(1)} %collective-permute-done.38.refs_14_), channel_id=1, source_target_pairs={{0,8},{1,5},{2,10},{3,7},{8,16},{9,1},{10,18},{11,3},{16,24},{17,9... | collective-permute-start | bytes 344072 | tf_op jit(solution)/shard_map/ppermute | solution.py:267
  60.4 4.9 %collective-permute-start.48 = (f32[112,256]{1,0:T(8,128)S(1)}, f32[112,256]{1,0:T(8,128)S(1)}, u32[]{:S(2)}, u32[]{:S(2)}) collective-permute-start(f32[112,256]{1,0:T(8,128)S(1)} %collective-permute-done.47.refs_17_), channel_id=1, source_target_pairs={{0,8},{1,5},{2,10},{3,7},{8,16},{9,1},{10,18},{11,3},{16,24},{17,9... | collective-permute-start | bytes 344072 | tf_op jit(solution)/shard_map/ppermute | solution.py:267
  61.7 4.9 %collective-permute-start.52 = (f32[112,256]{1,0:T(8,128)S(1)}, f32[112,256]{1,0:T(8,128)S(1)}, u32[]{:S(2)}, u32[]{:S(2)}) collective-permute-start(f32[112,256]{1,0:T(8,128)S(1)} %collective-permute-done.51.refs_18_), channel_id=1, source_target_pairs={{0,8},{1,5},{2,10},{3,7},{8,16},{9,1},{10,18},{11,3},{16,24},{17,9... | collective-permute-start | bytes 344072 | tf_op jit(solution)/shard_map/ppermute | solution.py:267
  62.9 4.9 %collective-permute-start.56 = (f32[112,256]{1,0:T(8,128)S(1)}, f32[112,256]{1,0:T(8,128)S(1)}, u32[]{:S(2)}, u32[]{:S(2)}) collective-permute-start(f32[112,256]{1,0:T(8,128)S(1)} %collective-permute-done.55.refs_19_), channel_id=1, source_target_pairs={{0,8},{1,5},{2,10},{3,7},{8,16},{9,1},{10,18},{11,3},{16,24},{17,9... | collective-permute-start | bytes 344072 | tf_op jit(solution)/shard_map/ppermute | solution.py:267
  69.0 20.3 %collective-permute-start.46 = (f32[112,256]{1,0:T(8,128)S(1)}, f32[112,256]{1,0:T(8,128)S(1)}, u32[]{:S(2)}, u32[]{:S(2)}) collective-permute-start(f32[112,256]{1,0:T(8,128)S(1)} %collective-permute-done.45.refs_24_), channel_id=1, source_target_pairs={{0,8},{1,5},{2,10},{3,7},{8,16},{9,1},{10,18},{11,3},{16,24},{17,9... | collective-permute-start | bytes 344072 | tf_op jit(solution)/shard_map/ppermute | solution.py:267
  70.3 19.1 %collective-permute-start.50 = (f32[112,256]{1,0:T(8,128)S(1)}, f32[112,256]{1,0:T(8,128)S(1)}, u32[]{:S(2)}, u32[]{:S(2)}) collective-permute-start(f32[112,256]{1,0:T(8,128)S(1)} %collective-permute-done.49.refs_25_), channel_id=1, source_target_pairs={{0,8},{1,5},{2,10},{3,7},{8,16},{9,1},{10,18},{11,3},{16,24},{17,9... | collective-permute-start | bytes 344072 | tf_op jit(solution)/shard_map/ppermute | solution.py:267
  71.5 17.9 %collective-permute-start.54 = (f32[112,256]{1,0:T(8,128)S(1)}, f32[112,256]{1,0:T(8,128)S(1)}, u32[]{:S(2)}, u32[]{:S(2)}) collective-permute-start(f32[112,256]{1,0:T(8,128)S(1)} %collective-permute-done.53.refs_26_), channel_id=1, source_target_pairs={{0,8},{1,5},{2,10},{3,7},{8,16},{9,1},{10,18},{11,3},{16,24},{17,9... | collective-permute-start | bytes 344072 | tf_op jit(solution)/shard_map/ppermute | solution.py:267
  72.7 16.7 %collective-permute-start.58 = (f32[112,256]{1,0:T(8,128)S(1)}, f32[112,256]{1,0:T(8,128)S(1)}, u32[]{:S(2)}, u32[]{:S(2)}) collective-permute-start(f32[112,256]{1,0:T(8,128)S(1)} %collective-permute-done.57.refs_27_), channel_id=1, source_target_pairs={{0,8},{1,5},{2,10},{3,7},{8,16},{9,1},{10,18},{11,3},{16,24},{17,9... | collective-permute-start | bytes 344072 | tf_op jit(solution)/shard_map/ppermute | solution.py:267
  74.2 6.4 %collective-permute-start.40 = (f32[8,128]{1,0:T(8,128)S(1)}, f32[8,128]{1,0:T(8,128)S(1)}, u32[]{:S(2)}, u32[]{:S(2)}) collective-permute-start(f32[8,128]{1,0:T(8,128)S(1)} %tally.1.refs_0_), channel_id=1, source_target_pairs={{0,28},{8,20},{16,12},{24,4},{28,0},{20,8},{12,16},{4,24},{1,29},{... | collective-permute-start | bytes 12296 | tf_op jit(solution)/shard_map/ppermute | solution.py:292
  (38 other events, 177.1 us)
where the time goes:
time: 90.8 us; the launch traced here: 90.7 us
  starting transfers between devices  73.2 us (81%)
  waiting for transfers between devices  9.27 us (10%)
  Pallas kernels  7.35 us (8%)
    ppermute x56, starting transfers between devices, hop(): return lax.ppermute(value, ('dp', 'mp'), perm)  69.4 us
    ppermute x3, waiting for transfers between devices, body(): arriving = lax.ppermute(table, axis, pairs)  7.36 us
    pallas_call x2, Pallas kernels, update(): pl.pallas_call(functools.partial(update_kernel, n, max_norm, pieces, len(...  5.28 us
    ppermute x3, starting transfers between devices, body(): arriving = lax.ppermute(table, axis, pairs)  3.78 us
    ppermute x56, waiting for transfers between devices, hop(): return lax.ppermute(value, ('dp', 'mp'), perm)  1.91 us
  transfers between devices with their start and end apart: 59, of which 26 were waited for; matrix products, arithmetic and copies ran while one was open for 0% of the time, Pallas kernels for 6%

commit v1 on v0

--- a/solution.py
+++ b/solution.py
@@ -14,7 +14,7 @@
 CLIP_LEVEL = 0.2
 EPSILON = 1e-06
 STREAMS = 4
-GAP = 4
+RIDER = 2
 LATE = 2
 VMEM = pl.BlockSpec(memory_space=pltpu.VMEM)
 SMEM = pl.BlockSpec(memory_space=pltpu.SMEM)
@@ -115,28 +115,24 @@
     )(got, *state)
 
 
-def tally_kernel(n, chunks, *refs):
+def tally_kernel(n, count, *refs):
     out = refs[-1]
-    place = lax.broadcasted_iota(jnp.int32, out.shape, 0)
-    table = jnp.zeros(out.shape, jnp.float32)
-    for back, positions in chunks:
-        squares = jnp.zeros((8, 128), jnp.float32)
-        for k in positions:
-            mean = refs[k][...] * (1.0 / n)
-            squares = squares + jnp.sum((mean * mean).reshape(-1, 8, 128), axis=0)
-        row = jnp.sum(squares, axis=0, keepdims=True)
-        table = jnp.where(place == chunk_index(n, back), row, table)
-    out[...] = table
-
-
-def tally(chunks, state, n):
-    pieces = [piece for chunk in chunks for piece in chunk]
-    count = len(chunks[0])
-    spans = [(chunk[0][0], range(count * k, count * (k + 1))) for k, chunk in enumerate(chunks)]
-    values = [sums for _, _, sums in pieces]
-    return pl.pallas_call(
-        functools.partial(tally_kernel, n, spans),
-        out_shape=jax.ShapeDtypeStruct((-(-n // 8) * 8, 128), jnp.float32),
+    squares = jnp.zeros((8, 128), jnp.float32)
+    for ref in refs[:count]:
+        mean = ref[...] * (1.0 / n)
+        squares = squares + jnp.sum((mean * mean).reshape(-1, 8, 128), axis=0)
+    row = jnp.sum(squares, axis=0, keepdims=True)
+    lane = 128 * lax.rem(lax.axis_index("mp"), 2)
+    place = lax.broadcasted_iota(jnp.int32, (out.shape[0], 128), 0)
+    out[...] = jnp.zeros_like(out)
+    out[:, pl.ds(pl.multiple_of(lane, 128), 128)] = jnp.where(place == chunk_index(n, 0), row, 0.0)
+
+
+def tally(values, state, n):
+    columns = values[0].shape[1]
+    return pl.pallas_call(
+        functools.partial(tally_kernel, n, len(values)),
+        out_shape=jax.ShapeDtypeStruct((-(-n // 8) * 8, columns), jnp.float32),
         in_specs=[VMEM] * (len(values) + len(state)),
         out_specs=VMEM,
         cost_estimate=estimate(sum(v.size for v in values), 40, 3),
@@ -145,20 +141,44 @@
     )(*values, *state)
 
 
-def sum_kernel(*refs):
-    refs[-1][...] = refs[0][...] + refs[1][...]
-
-
-def sum_small(a, b, state):
-    return pl.pallas_call(
-        sum_kernel,
-        out_shape=jax.ShapeDtypeStruct(a.shape, jnp.float32),
-        in_specs=[VMEM] * (2 + len(state)),
-        out_specs=VMEM,
-        cost_estimate=estimate(a.size, 12, 1),
-        compiler_params=grant(0),
-        name="sum",
-    )(a, b, *state)
+def merge_kernel(how, count, *refs):
+    table = refs[0][...]
+    for ref in refs[1:count]:
+        other = ref[ref.shape[0] - table.shape[0] :, :]
+        table = table + other if how == "sum" else jnp.maximum(table, other)
+    refs[-1][...] = table
+
+
+def merge(tables, state, how):
+    return pl.pallas_call(
+        functools.partial(merge_kernel, how, len(tables)),
+        out_shape=jax.ShapeDtypeStruct(tables[0].shape, jnp.float32),
+        in_specs=[VMEM] * (len(tables) + len(state)),
+        out_specs=VMEM,
+        cost_estimate=estimate(tables[0].size, 12, 1),
+        compiler_params=grant(0),
+        name="merge",
+    )(*tables, *state)
+
+
+def load_kernel(piece_ref, table_ref, other_ref, *refs):
+    out = refs[-1]
+    rows = piece_ref.shape[0]
+    out[:rows, :] = piece_ref[...]
+    out[rows:, :] = jnp.maximum(table_ref[...], other_ref[...])
+
+
+def load_rider(piece, table, other, state):
+    shape = (piece.shape[0] + table.shape[0], piece.shape[1])
+    return pl.pallas_call(
+        load_kernel,
+        out_shape=jax.ShapeDtypeStruct(shape, jnp.float32),
+        in_specs=[VMEM] * (3 + len(state)),
+        out_specs=VMEM,
+        cost_estimate=estimate(piece.size, 12, 1),
+        compiler_params=grant(0),
+        name="load",
+    )(piece, table, other, *state)
 
 
 def update_kernel(n, max_norm, pieces, n_outs, total_ref, slow_ref, momentum_ref, *refs):
@@ -173,7 +193,7 @@
     for k, (back, start, rows) in enumerate(pieces):
         index = chunk_index(n, back)
         here, there = pl.ds(start, rows), pl.ds(at, rows)
-        gradient = factor * (sums[k][...] * (1.0 / n))
+        gradient = factor * (sums[k][:rows, :] * (1.0 / n))
         momentum_next = MOMENTUM_RATE * momentum_ref[index, here] + gradient
         slow_next = slow_ref[index, here] - OUTER_RATE * (gradient + MOMENTUM_RATE * momentum_next)
         slow_buf[there] = slow_next
@@ -233,22 +253,21 @@
     return perm
 
 
+def rides(n, m):
+    return n % 2 == 0 and m > 1 and m & (m - 1) == 0
+
+
 def exchanges(n, m):
-    order = ring_order(n)
-    across = None if n % 2 else [(order[k], order[(k + n // 2) % n]) for k in range(n)]
-    steps = [("dp", across)]
-    if m & (m - 1):
-        return steps + [("mp", None)]
-    bit = 1
+    hops = STREAMS * (n - 1)
+    arrived = STREAMS * (1 + n // 2) + RIDER
+    swap = [(c, c ^ 1) for c in range(m)]
+    steps = [(swap, STREAMS, STREAMS + RIDER), (swap, arrived + 1, arrived + 3)]
+    bit = 2
     while bit < m:
-        steps.append(("mp", [(i, i ^ bit) for i in range(m)]))
+        start = steps[-1][2]
+        steps.append(([(c, c ^ bit) for c in range(m)], start, min(start + STREAMS - 1, hops)))
         bit *= 2
     return steps
-
-
-def exchange_slots(n, m):
-    count = len(exchanges(n, m))
-    return [STREAMS * (n - 1) - GAP * (count - j) for j in range(count)]
 
 
 def body(slow_weights, fast_weights, momentum):
@@ -261,7 +280,8 @@
     moment = momentum.reshape(n, depth, columns)
     parts = split(depth)
     perm = ring_perm(n, m)
-    steps, slots = exchanges(n, m), exchange_slots(n, m)
+    riding = rides(n, m)
+    steps = exchanges(n, m) if riding else []
 
     def hop(value):
         return lax.ppermute(value, ("dp", "mp"), perm)
@@ -275,26 +295,32 @@
 
     state = (slow, moment)
     chunks = [[(0, part, held[s]) for s, part in enumerate(parts)]]
-    table, arriving = None, None
-    for slot in range(STREAMS * (n - 1)):
+    table = tally([sums for _, _, sums in chunks[0]], state, n)
+    if not riding:
+        table = lax.psum(table, ("dp", "mp"))
+    got = [None] * len(steps)
+
+    def swap(j, value):
+        return lax.ppermute(value, "mp", steps[j][0])
+
+    for slot in range(STREAMS * (n - 1) + 1):
         step, s = divmod(slot, STREAMS)
-        if slot in slots:
-            j = slots.index(slot)
-            if j == 0:
-                known = 1 if n % 2 else n // 2
-                table = tally(chunks[:known], state, n)
-            else:
-                table = sum_small(table, arriving, state)
-            axis, pairs = steps[j]
-            if pairs is None:
-                arriving = lax.psum(table, axis) - table
-            else:
-                arriving = lax.ppermute(table, axis, pairs)
+        for j, (_, start, end) in enumerate(steps):
+            if slot == end and j == 0:
+                held[s] = load_rider(held[s], table, got[j], state)
+            elif slot == end:
+                table = merge([table, got[j]], state, "max" if j == 1 else "sum")
+            if slot == start:
+                if j == 1:
+                    riders = [chunk[RIDER][2] for chunk in chunks[2 : 2 + n // 2]]
+                    table = merge([table, got[0]] + riders, state, "max")
+                got[j] = swap(j, table)
+        if step == n - 1:
+            break
         held[s] = hop(held[s])
         if s == 0:
             chunks.append([])
         chunks[-1].append((step + 1, parts[s], held[s]))
-    table = sum_small(table, arriving, state)
 
     mine = [piece for chunk in chunks[:-1] for piece in chunk]
     outs = update(table, mine, slow, moment, (), n, max_norm)

time: 90.8 us -> 89.1 us (0.981)
  local copies, waits for them, and re-layouts: 0.01 us -> 3.55 us
  starting transfers between devices: 73.2 us -> 69.7 us
  waiting for transfers between devices: 9.27 us -> 7.75 us
    unnamed x6 -> x10, local copies, waits for them, and re-layouts: 0.01 us -> 3.55 us
    ppermute x3, waiting for transfers between devices: 7.36 us -> 4.48 us  [swap(): return lax.ppermute(value, 'mp', steps[j][0])]
    ppermute x3, starting transfers between devices: 3.78 us -> 1.56 us  [swap(): return lax.ppermute(value, 'mp', steps[j][0])]
    ppermute x56, waiting for transfers between devices: 1.91 us -> 3.27 us  [hop(): return lax.ppermute(value, ('dp', 'mp'), perm)]
    ppermute x56, starting transfers between devices: 69.4 us -> 68.2 us  [hop(): return lax.ppermute(value, ('dp', 'mp'), perm)]
  transfers between devices with their start and end apart: 59 -> 59, of which waited for: 26 -> 23; matrix products, arithmetic and copies ran while one was open for 0% -> 0% of each run, Pallas kernels for 6% -> 6%
where the time goes in v1:
time: 89.1 us; the launch traced here: 88.8 us
  starting transfers between devices  69.7 us (78%)
  waiting for transfers between devices  7.75 us (9%)
  Pallas kernels  6.87 us (8%)
  local copies, waits for them, and re-layouts  3.55 us (4%)
  between operations  0.92 us (1%)
    ppermute x56, starting transfers between devices, hop(): return lax.ppermute(value, ('dp', 'mp'), perm)  68.2 us
    pallas_call x2, Pallas kernels, update(): pl.pallas_call(functools.partial(update_kernel, n, max_norm, pieces, len(...  5.28 us
    ppermute x3, waiting for transfers between devices, swap(): return lax.ppermute(value, 'mp', steps[j][0])  4.48 us
    unnamed x10, local copies, waits for them, and re-layouts  3.55 us
    ppermute x56, waiting for transfers between devices, hop(): return lax.ppermute(value, ('dp', 'mp'), perm)  3.27 us
  transfers between devices with their start and end apart: 59, of which 23 were waited for; matrix products, arithmetic and copies ran while one was open for 0% of the time, Pallas kernels for 6%

profile of v1, /device:TPU:0, one launch (start us, length us, event | category | flops | bytes accessed | tf_op | source)
XLA Modules:
  0.0 88.8 jit_solution(10796862769571712061)
XLA Ops:
  0.6 2.0 %copy-done = f32[1,3584,256]{2,1,0:T(8,128)S(1)} copy-done((f32[1,3584,256]{2,1,0:T(8,128)S(1)}, f32[1,3584,256]{2,1,0:T(8,128)}, u32[]{:S(2)}) %copy-start) | copy-done | bytes 3670040
  2.7 1.5 %copy-done.3 = bf16[1,1,3584,256]{3,2,1,0:T(8,128)(2,1)S(1)} copy-done((bf16[1,1,3584,256]{3,2,1,0:T(8,128)(2,1)S(1)}, bf16[1,1,3584,256]{3,2,1,0:T(8,128)(2,1)}, u32[]{:S(2)}) %copy-start.3) | copy-done | bytes 1835032
  4.2 3.1 %collective-permute-start.14 = (f32[112,256]{1,0:T(8,128)S(1)}, f32[112,256]{1,0:T(8,128)S(1)}, u32[]{:S(2)}, u32[]{:S(2)}) collective-permute-start(f32[112,256]{1,0:T(8,128)S(1)} %own.4), channel_id=1, source_target_pairs={{0,8},{1,5},{2,10},{3,7},{8,16},{9,1},{10,18},{11,3},{16,24},{17,9... | collective-permute-start | bytes 344072 | tf_op jit(solution)/shard_map/ppermute | solution.py:287
  8.3 1.6 %collective-permute-start = (f32[112,256]{1,0:T(8,128)S(1)}, f32[112,256]{1,0:T(8,128)S(1)}, u32[]{:S(2)}, u32[]{:S(2)}) collective-permute-start(f32[112,256]{1,0:T(8,128)S(1)} %first.1), channel_id=1, source_target_pairs={{0,8},{1,5},{2,10},{3,7},{8,16},{9,1},{10,18},{11,3},{16,24},{17,9... | collective-permute-start | bytes 344072 | tf_op jit(solution)/shard_map/ppermute | solution.py:287
  9.9 1.6 %collective-permute-start.7 = (f32[112,256]{1,0:T(8,128)S(1)}, f32[112,256]{1,0:T(8,128)S(1)}, u32[]{:S(2)}, u32[]{:S(2)}) collective-permute-start(f32[112,256]{1,0:T(8,128)S(1)} %own.3), channel_id=1, source_target_pairs={{0,8},{1,5},{2,10},{3,7},{8,16},{9,1},{10,18},{11,3},{16,24},{17,9... | collective-permute-start | bytes 344072 | tf_op jit(solution)/shard_map/ppermute | solution.py:287
  11.5 1.6 %collective-permute-start.21 = (f32[112,256]{1,0:T(8,128)S(1)}, f32[112,256]{1,0:T(8,128)S(1)}, u32[]{:S(2)}, u32[]{:S(2)}) collective-permute-start(f32[112,256]{1,0:T(8,128)S(1)} %own.5), channel_id=1, source_target_pairs={{0,8},{1,5},{2,10},{3,7},{8,16},{9,1},{10,18},{11,3},{16,24},{17,9... | collective-permute-start | bytes 344072 | tf_op jit(solution)/shard_map/ppermute | solution.py:287
  14.9 1.5 %collective-permute-start.8 = (f32[112,256]{1,0:T(8,128)S(1)}, f32[112,256]{1,0:T(8,128)S(1)}, u32[]{:S(2)}, u32[]{:S(2)}) collective-permute-start(f32[112,256]{1,0:T(8,128)S(1)} %add.35), channel_id=1, source_target_pairs={{0,8},{1,5},{2,10},{3,7},{8,16},{9,1},{10,18},{11,3},{16,24},{17,9... | collective-permute-start | bytes 344072 | tf_op jit(solution)/shard_map/ppermute | solution.py:287
  16.4 1.6 %collective-permute-start.22 = (f32[112,256]{1,0:T(8,128)S(1)}, f32[112,256]{1,0:T(8,128)S(1)}, u32[]{:S(2)}, u32[]{:S(2)}) collective-permute-start(f32[112,256]{1,0:T(8,128)S(1)} %add.49), channel_id=1, source_target_pairs={{0,8},{1,5},{2,10},{3,7},{8,16},{9,1},{10,18},{11,3},{16,24},{17,9... | collective-permute-start | bytes 344072 | tf_op jit(solution)/shard_map/ppermute | solution.py:287
  18.1 1.2 %collective-permute-start.16 = (f32[112,256]{1,0:T(8,128)S(1)}, f32[112,256]{1,0:T(8,128)S(1)}, u32[]{:S(2)}, u32[]{:S(2)}) collective-permute-start(f32[112,256]{1,0:T(8,128)S(1)} %add.43), channel_id=1, source_target_pairs={{0,8},{1,5},{2,10},{3,7},{8,16},{9,1},{10,18},{11,3},{16,24},{17,9... | collective-permute-start | bytes 344072 | tf_op jit(solution)/shard_map/ppermute | solution.py:287
  19.3 1.2 %collective-permute-start.2 = (f32[112,256]{1,0:T(8,128)S(1)}, f32[112,256]{1,0:T(8,128)S(1)}, u32[]{:S(2)}, u32[]{:S(2)}) collective-permute-start(f32[112,256]{1,0:T(8,128)S(1)} %add.29), channel_id=1, source_target_pairs={{0,8},{1,5},{2,10},{3,7},{8,16},{9,1},{10,18},{11,3},{16,24},{17,9... | collective-permute-start | bytes 344072 | tf_op jit(solution)/shard_map/ppermute | solution.py:287
  20.5 1.2 %collective-permute-start.9 = (f32[112,256]{1,0:T(8,128)S(1)}, f32[112,256]{1,0:T(8,128)S(1)}, u32[]{:S(2)}, u32[]{:S(2)}) collective-permute-start(f32[112,256]{1,0:T(8,128)S(1)} %add.36), channel_id=1, source_target_pairs={{0,8},{1,5},{2,10},{3,7},{8,16},{9,1},{10,18},{11,3},{16,24},{17,9... | collective-permute-start | bytes 344072 | tf_op jit(solution)/shard_map/ppermute | solution.py:287
  21.8 1.2 %collective-permute-start.23 = (f32[112,256]{1,0:T(8,128)S(1)}, f32[112,256]{1,0:T(8,128)S(1)}, u32[]{:S(2)}, u32[]{:S(2)}) collective-permute-start(f32[112,256]{1,0:T(8,128)S(1)} %add.50), channel_id=1, source_target_pairs={{0,8},{1,5},{2,10},{3,7},{8,16},{9,1},{10,18},{11,3},{16,24},{17,9... | collective-permute-start | bytes 344072 | tf_op jit(solution)/shard_map/ppermute | solution.py:287
  23.0 1.2 %collective-permute-start.17 = (f32[112,256]{1,0:T(8,128)S(1)}, f32[112,256]{1,0:T(8,128)S(1)}, u32[]{:S(2)}, u32[]{:S(2)}) collective-permute-start(f32[112,256]{1,0:T(8,128)S(1)} %add.44), channel_id=1, source_target_pairs={{0,8},{1,5},{2,10},{3,7},{8,16},{9,1},{10,18},{11,3},{16,24},{17,9... | collective-permute-start | bytes 344072 | tf_op jit(solution)/shard_map/ppermute | solution.py:287
  27.9 1.2 %collective-permute-start.18 = (f32[112,256]{1,0:T(8,128)S(1)}, f32[112,256]{1,0:T(8,128)S(1)}, u32[]{:S(2)}, u32[]{:S(2)}) collective-permute-start(f32[112,256]{1,0:T(8,128)S(1)} %add.45), channel_id=1, source_target_pairs={{0,8},{1,5},{2,10},{3,7},{8,16},{9,1},{10,18},{11,3},{16,24},{17,9... | collective-permute-start | bytes 344072 | tf_op jit(solution)/shard_map/ppermute | solution.py:287
  29.1 1.2 %collective-permute-start.4 = (f32[112,256]{1,0:T(8,128)S(1)}, f32[112,256]{1,0:T(8,128)S(1)}, u32[]{:S(2)}, u32[]{:S(2)}) collective-permute-start(f32[112,256]{1,0:T(8,128)S(1)} %add.31), channel_id=1, source_target_pairs={{0,8},{1,5},{2,10},{3,7},{8,16},{9,1},{10,18},{11,3},{16,24},{17,9... | collective-permute-start | bytes 344072 | tf_op jit(solution)/shard_map/ppermute | solution.py:287
  30.4 1.2 %collective-permute-start.11 = (f32[112,256]{1,0:T(8,128)S(1)}, f32[112,256]{1,0:T(8,128)S(1)}, u32[]{:S(2)}, u32[]{:S(2)}) collective-permute-start(f32[112,256]{1,0:T(8,128)S(1)} %add.38), channel_id=1, source_target_pairs={{0,8},{1,5},{2,10},{3,7},{8,16},{9,1},{10,18},{11,3},{16,24},{17,9... | collective-permute-start | bytes 344072 | tf_op jit(solution)/shard_map/ppermute | solution.py:287
  31.6 1.2 %collective-permute-start.25 = (f32[112,256]{1,0:T(8,128)S(1)}, f32[112,256]{1,0:T(8,128)S(1)}, u32[]{:S(2)}, u32[]{:S(2)}) collective-permute-start(f32[112,256]{1,0:T(8,128)S(1)} %add.52), channel_id=1, source_target_pairs={{0,8},{1,5},{2,10},{3,7},{8,16},{9,1},{10,18},{11,3},{16,24},{17,9... | collective-permute-start | bytes 344072 | tf_op jit(solution)/shard_map/ppermute | solution.py:287
  34.1 1.2 %collective-permute-start.5 = (f32[112,256]{1,0:T(8,128)S(1)}, f32[112,256]{1,0:T(8,128)S(1)}, u32[]{:S(2)}, u32[]{:S(2)}) collective-permute-start(f32[112,256]{1,0:T(8,128)S(1)} %add.32), channel_id=1, source_target_pairs={{0,8},{1,5},{2,10},{3,7},{8,16},{9,1},{10,18},{11,3},{16,24},{17,9... | collective-permute-start | bytes 344072 | tf_op jit(solution)/shard_map/ppermute | solution.py:287
  35.3 1.2 %collective-permute-start.12 = (f32[112,256]{1,0:T(8,128)S(1)}, f32[112,256]{1,0:T(8,128)S(1)}, u32[]{:S(2)}, u32[]{:S(2)}) collective-permute-start(f32[112,256]{1,0:T(8,128)S(1)} %add.39), channel_id=1, source_target_pairs={{0,8},{1,5},{2,10},{3,7},{8,16},{9,1},{10,18},{11,3},{16,24},{17,9... | collective-permute-start | bytes 344072 | tf_op jit(solution)/shard_map/ppermute | solution.py:287
  52.5 1.4 %collective-permute-done.30.refs_2_.refs_10_ = f32[120,256]{1,0:T(8,128)S(1)} collective-permute-done((f32[120,256]{1,0:T(8,128)S(1)}, f32[120,256]{1,0:T(8,128)S(1)}, u32[]{:S(2)}, u32[]{:S(2)}) %collective-permute-start.30) | collective-permute-done | bytes 122912 | tf_op jit(solution)/shard_map/ppermute | solution.py:287
  79.9 1.5 %collective-permute-start.35 = (f32[8,256]{1,0:T(8,128)S(1)}, f32[8,256]{1,0:T(8,128)S(1)}, u32[]{:S(2)}, u32[]{:S(2)}) collective-permute-start(f32[8,256]{1,0:T(8,128)S(1)} %merge.4.refs_0_), channel_id=1, source_target_pairs={{0,2},{1,3},{2,0},{3,1},{4,6},{5,7},{6,4},{7,5},{8,10},{9,11},{10,... | collective-permute-start | bytes 24584 | tf_op jit(solution)/shard_map/ppermute | solution.py:304
  81.3 2.2 %collective-permute-done.35.refs_1_ = f32[8,256]{1,0:T(8,128)S(1)} collective-permute-done((f32[8,256]{1,0:T(8,128)S(1)}, f32[8,256]{1,0:T(8,128)S(1)}, u32[]{:S(2)}, u32[]{:S(2)}) %collective-permute-start.35) | collective-permute-done | bytes 8224 | tf_op jit(solution)/shard_map/ppermute | solution.py:304
  83.5 4.0 %update.2 = (f32[8,448,256]{2,1,0:T(8,128)}, f32[8,448,256]{2,1,0:T(8,128)}, bf16[8,448,256]{2,1,0:T(8,128)(2,1)}) custom-call(f32[8,256]{1,0:T(8,128)S(1)} %merge.5.total_ref, f32[8,448,256]{2,1,0:T(8,128)S(1)} %bitcast.43, f32[8,448,256]{2,1,0:T(8,128)S(1)} %bitcast.70, f32[112,256]{1,0:T(8,128)S(1)} %add.34.refs_0_, f32[112,256]{1,0:T(8,128)S(1)} %add.41.refs_1_, ...), custom_call_target="tpu_custom_call" | custom-call | flops 6422528 | bytes 17661952 | tf_op jit(solution)/shard_map/update/pallas_call | solution.py:218
  87.6 1.3 %update.3 = (f32[8,448,256]{2,1,0:T(8,128)}, f32[8,448,256]{2,1,0:T(8,128)}, bf16[8,448,256]{2,1,0:T(8,128)(2,1)}) custom-call(f32[8,256]{1,0:T(8,128)S(1)} %merge.5.total_ref, f32[8,448,256]{2,1,0:T(8,128)S(1)} %bitcast.44, f32[8,448,256]{2,1,0:T(8,128)S(1)} %bitcast.71, ...), custom_call_target="tpu_custom_call", output_to_operand_aliasing={{0}: (7, {}), {1}: (8, {}), {2}: (9, {})} | custom-call | flops 917504 | bytes 2523136 | tf_op jit(solution)/shard_map/update/pallas_call | solution.py:218
  (143 shorter events, 49.8 us)
Async XLA Ops:
  4.2 9.0 %collective-permute-start.14 = (f32[112,256]{1,0:T(8,128)S(1)}, f32[112,256]{1,0:T(8,128)S(1)}, u32[]{:S(2)}, u32[]{:S(2)}) collective-permute-start(f32[112,256]{1,0:T(8,128)S(1)} %own.4), channel_id=1, source_target_pairs={{0,8},{1,5},{2,10},{3,7},{8,16},{9,1},{10,18},{11,3},{16,24},{17,9... | collective-permute-start | bytes 344072 | tf_op jit(solution)/shard_map/ppermute | solution.py:287
  8.3 5.7 %collective-permute-start = (f32[112,256]{1,0:T(8,128)S(1)}, f32[112,256]{1,0:T(8,128)S(1)}, u32[]{:S(2)}, u32[]{:S(2)}) collective-permute-start(f32[112,256]{1,0:T(8,128)S(1)} %first.1), channel_id=1, source_target_pairs={{0,8},{1,5},{2,10},{3,7},{8,16},{9,1},{10,18},{11,3},{16,24},{17,9... | collective-permute-start | bytes 344072 | tf_op jit(solution)/shard_map/ppermute | solution.py:287
  9.9 5.0 %collective-permute-start.7 = (f32[112,256]{1,0:T(8,128)S(1)}, f32[112,256]{1,0:T(8,128)S(1)}, u32[]{:S(2)}, u32[]{:S(2)}) collective-permute-start(f32[112,256]{1,0:T(8,128)S(1)} %own.3), channel_id=1, source_target_pairs={{0,8},{1,5},{2,10},{3,7},{8,16},{9,1},{10,18},{11,3},{16,24},{17,9... | collective-permute-start | bytes 344072 | tf_op jit(solution)/shard_map/ppermute | solution.py:287
  13.9 5.4 %collective-permute-start.1 = (f32[112,256]{1,0:T(8,128)S(1)}, f32[112,256]{1,0:T(8,128)S(1)}, u32[]{:S(2)}, u32[]{:S(2)}) collective-permute-start(f32[112,256]{1,0:T(8,128)S(1)} %add.28), channel_id=1, source_target_pairs={{0,8},{1,5},{2,10},{3,7},{8,16},{9,1},{10,18},{11,3},{16,24},{17,9... | collective-permute-start | bytes 344072 | tf_op jit(solution)/shard_map/ppermute | solution.py:287
  14.9 5.6 %collective-permute-start.8 = (f32[112,256]{1,0:T(8,128)S(1)}, f32[112,256]{1,0:T(8,128)S(1)}, u32[]{:S(2)}, u32[]{:S(2)}) collective-permute-start(f32[112,256]{1,0:T(8,128)S(1)} %add.35), channel_id=1, source_target_pairs={{0,8},{1,5},{2,10},{3,7},{8,16},{9,1},{10,18},{11,3},{16,24},{17,9... | collective-permute-start | bytes 344072 | tf_op jit(solution)/shard_map/ppermute | solution.py:287
  16.4 5.3 %collective-permute-start.22 = (f32[112,256]{1,0:T(8,128)S(1)}, f32[112,256]{1,0:T(8,128)S(1)}, u32[]{:S(2)}, u32[]{:S(2)}) collective-permute-start(f32[112,256]{1,0:T(8,128)S(1)} %add.49), channel_id=1, source_target_pairs={{0,8},{1,5},{2,10},{3,7},{8,16},{9,1},{10,18},{11,3},{16,24},{17,9... | collective-permute-start | bytes 344072 | tf_op jit(solution)/shard_map/ppermute | solution.py:287
  42.7 6.2 %collective-permute-start.29 = (f32[112,256]{1,0:T(8,128)S(1)}, f32[112,256]{1,0:T(8,128)S(1)}, u32[]{:S(2)}, u32[]{:S(2)}) collective-permute-start(f32[112,256]{1,0:T(8,128)S(1)} %add.48.refs_2_), channel_id=1, source_target_pairs={{0,8},{1,5},{2,10},{3,7},{8,16},{9,1},{10,18},{11,3},{16,24},{17,9... | collective-permute-start | bytes 344072 | tf_op jit(solution)/shard_map/ppermute | solution.py:287
  43.9 6.2 %collective-permute-start.36 = (f32[112,256]{1,0:T(8,128)S(1)}, f32[112,256]{1,0:T(8,128)S(1)}, u32[]{:S(2)}, u32[]{:S(2)}) collective-permute-start(f32[112,256]{1,0:T(8,128)S(1)} %add.34.refs_0_), channel_id=1, source_target_pairs={{0,8},{1,5},{2,10},{3,7},{8,16},{9,1},{10,18},{11,3},{16,24},{17,9... | collective-permute-start | bytes 344072 | tf_op jit(solution)/shard_map/ppermute | solution.py:287
  45.1 6.1 %collective-permute-start.43 = (f32[112,256]{1,0:T(8,128)S(1)}, f32[112,256]{1,0:T(8,128)S(1)}, u32[]{:S(2)}, u32[]{:S(2)}) collective-permute-start(f32[112,256]{1,0:T(8,128)S(1)} %add.41.refs_1_), channel_id=1, source_target_pairs={{0,8},{1,5},{2,10},{3,7},{8,16},{9,1},{10,18},{11,3},{16,24},{17,9... | collective-permute-start | bytes 344072 | tf_op jit(solution)/shard_map/ppermute | solution.py:287
  46.3 5.6 %collective-permute-start.52 = (f32[112,256]{1,0:T(8,128)S(1)}, f32[112,256]{1,0:T(8,128)S(1)}, u32[]{:S(2)}, u32[]{:S(2)}) collective-permute-start(f32[112,256]{1,0:T(8,128)S(1)} %add.55.refs_3_), channel_id=1, source_target_pairs={{0,8},{1,5},{2,10},{3,7},{8,16},{9,1},{10,18},{11,3},{16,24},{17,9... | collective-permute-start | bytes 344072 | tf_op jit(solution)/shard_map/ppermute | solution.py:287
  51.2 5.0 %collective-permute-start.44 = (f32[112,256]{1,0:T(8,128)S(1)}, f32[112,256]{1,0:T(8,128)S(1)}, u32[]{:S(2)}, u32[]{:S(2)}) collective-permute-start(f32[112,256]{1,0:T(8,128)S(1)} %collective-permute-done.43.refs_5_), channel_id=1, source_target_pairs={{0,8},{1,5},{2,10},{3,7},{8,16},{9,1},{10,18},{11,3},{16,24},{17,9... | collective-permute-start | bytes 344072 | tf_op jit(solution)/shard_map/ppermute | solution.py:287
  51.9 5.6 %collective-permute-start.53 = (f32[112,256]{1,0:T(8,128)S(1)}, f32[112,256]{1,0:T(8,128)S(1)}, u32[]{:S(2)}, u32[]{:S(2)}) collective-permute-start(f32[112,256]{1,0:T(8,128)S(1)} %collective-permute-done.52.refs_7_), channel_id=1, source_target_pairs={{0,8},{1,5},{2,10},{3,7},{8,16},{9,1},{10,18},{11,3},{16,24},{17,9... | collective-permute-start | bytes 344072 | tf_op jit(solution)/shard_map/ppermute | solution.py:287
  53.8 5.0 %collective-permute-start.31 = (f32[120,256]{1,0:T(8,128)S(1)}, f32[120,256]{1,0:T(8,128)S(1)}, u32[]{:S(2)}, u32[]{:S(2)}) collective-permute-start(f32[120,256]{1,0:T(8,128)S(1)} %collective-permute-done.30.refs_2_.refs_10_), channel_id=1, source_target_pairs={{0,8},{1,5},{2,10},{3,7},{8,16},{9,1},{10,18},{11,3},{16,24},{17,9... | collective-permute-start | bytes 368648 | tf_op jit(solution)/shard_map/ppermute | solution.py:287
  56.3 5.0 %collective-permute-start.45 = (f32[112,256]{1,0:T(8,128)S(1)}, f32[112,256]{1,0:T(8,128)S(1)}, u32[]{:S(2)}, u32[]{:S(2)}) collective-permute-start(f32[112,256]{1,0:T(8,128)S(1)} %collective-permute-done.44.refs_9_), channel_id=1, source_target_pairs={{0,8},{1,5},{2,10},{3,7},{8,16},{9,1},{10,18},{11,3},{16,24},{17,9... | collective-permute-start | bytes 344072 | tf_op jit(solution)/shard_map/ppermute | solution.py:287
  57.5 5.0 %collective-permute-start.54 = (f32[112,256]{1,0:T(8,128)S(1)}, f32[112,256]{1,0:T(8,128)S(1)}, u32[]{:S(2)}, u32[]{:S(2)}) collective-permute-start(f32[112,256]{1,0:T(8,128)S(1)} %collective-permute-done.53.refs_11_), channel_id=1, source_target_pairs={{0,8},{1,5},{2,10},{3,7},{8,16},{9,1},{10,18},{11,3},{16,24},{17,9... | collective-permute-start | bytes 344072 | tf_op jit(solution)/shard_map/ppermute | solution.py:287
  58.8 5.0 %collective-permute-start.32 = (f32[120,256]{1,0:T(8,128)S(1)}, f32[120,256]{1,0:T(8,128)S(1)}, u32[]{:S(2)}, u32[]{:S(2)}) collective-permute-start(f32[120,256]{1,0:T(8,128)S(1)} %collective-permute-done.31.refs_3_.refs_14_), channel_id=1, source_target_pairs={{0,8},{1,5},{2,10},{3,7},{8,16},{9,1},{10,18},{11,3},{16,24},{17,9... | collective-permute-start | bytes 368648 | tf_op jit(solution)/shard_map/ppermute | solution.py:287
  60.1 5.0 %collective-permute-start.39 = (f32[112,256]{1,0:T(8,128)S(1)}, f32[112,256]{1,0:T(8,128)S(1)}, u32[]{:S(2)}, u32[]{:S(2)}) collective-permute-start(f32[112,256]{1,0:T(8,128)S(1)} %collective-permute-done.38.refs_12_), channel_id=1, source_target_pairs={{0,8},{1,5},{2,10},{3,7},{8,16},{9,1},{10,18},{11,3},{16,24},{17,9... | collective-permute-start | bytes 344072 | tf_op jit(solution)/shard_map/ppermute | solution.py:287
  62.5 5.0 %collective-permute-start.55 = (f32[112,256]{1,0:T(8,128)S(1)}, f32[112,256]{1,0:T(8,128)S(1)}, u32[]{:S(2)}, u32[]{:S(2)}) collective-permute-start(f32[112,256]{1,0:T(8,128)S(1)} %collective-permute-done.54.refs_15_), channel_id=1, source_target_pairs={{0,8},{1,5},{2,10},{3,7},{8,16},{9,1},{10,18},{11,3},{16,24},{17,9... | collective-permute-start | bytes 344072 | tf_op jit(solution)/shard_map/ppermute | solution.py:287
  65.1 5.0 %collective-permute-start.40 = (f32[112,256]{1,0:T(8,128)S(1)}, f32[112,256]{1,0:T(8,128)S(1)}, u32[]{:S(2)}, u32[]{:S(2)}) collective-permute-start(f32[112,256]{1,0:T(8,128)S(1)} %collective-permute-done.39.refs_16_), channel_id=1, source_target_pairs={{0,8},{1,5},{2,10},{3,7},{8,16},{9,1},{10,18},{11,3},{16,24},{17,9... | collective-permute-start | bytes 344072 | tf_op jit(solution)/shard_map/ppermute | solution.py:287
  71.3 5.0 %collective-permute-start.48 = (f32[112,256]{1,0:T(8,128)S(1)}, f32[112,256]{1,0:T(8,128)S(1)}, u32[]{:S(2)}, u32[]{:S(2)}) collective-permute-start(f32[112,256]{1,0:T(8,128)S(1)} %collective-permute-done.47.refs_21_), channel_id=1, source_target_pairs={{0,8},{1,5},{2,10},{3,7},{8,16},{9,1},{10,18},{11,3},{16,24},{17,9... | collective-permute-start | bytes 344072 | tf_op jit(solution)/shard_map/ppermute | solution.py:287
  73.8 13.7 %collective-permute-start.51 = (f32[120,256]{1,0:T(8,128)S(1)}, f32[120,256]{1,0:T(8,128)S(1)}, u32[]{:S(2)}, u32[]{:S(2)}) collective-permute-start(f32[120,256]{1,0:T(8,128)S(1)} %collective-permute-done.50.refs_26_), channel_id=1, source_target_pairs={{0,8},{1,5},{2,10},{3,7},{8,16},{9,1},{10,18},{11,3},{16,24},{17,9... | collective-permute-start | bytes 368648 | tf_op jit(solution)/shard_map/ppermute | solution.py:287
  75.1 12.5 %collective-permute-start.42 = (f32[112,256]{1,0:T(8,128)S(1)}, f32[112,256]{1,0:T(8,128)S(1)}, u32[]{:S(2)}, u32[]{:S(2)}) collective-permute-start(f32[112,256]{1,0:T(8,128)S(1)} %collective-permute-done.41.refs_24_), channel_id=1, source_target_pairs={{0,8},{1,5},{2,10},{3,7},{8,16},{9,1},{10,18},{11,3},{16,24},{17,9... | collective-permute-start | bytes 344072 | tf_op jit(solution)/shard_map/ppermute | solution.py:287
  76.3 11.3 %collective-permute-start.49 = (f32[112,256]{1,0:T(8,128)S(1)}, f32[112,256]{1,0:T(8,128)S(1)}, u32[]{:S(2)}, u32[]{:S(2)}) collective-permute-start(f32[112,256]{1,0:T(8,128)S(1)} %collective-permute-done.48.refs_25_), channel_id=1, source_target_pairs={{0,8},{1,5},{2,10},{3,7},{8,16},{9,1},{10,18},{11,3},{16,24},{17,9... | collective-permute-start | bytes 344072 | tf_op jit(solution)/shard_map/ppermute | solution.py:287
  77.5 10.1 %collective-permute-start.58 = (f32[112,256]{1,0:T(8,128)S(1)}, f32[112,256]{1,0:T(8,128)S(1)}, u32[]{:S(2)}, u32[]{:S(2)}) collective-permute-start(f32[112,256]{1,0:T(8,128)S(1)} %collective-permute-done.57.refs_27_), channel_id=1, source_target_pairs={{0,8},{1,5},{2,10},{3,7},{8,16},{9,1},{10,18},{11,3},{16,24},{17,9... | collective-permute-start | bytes 344072 | tf_op jit(solution)/shard_map/ppermute | solution.py:287
  (40 other events, 180.9 us)

commit v2 on v1

--- a/solution.py
+++ b/solution.py
@@ -14,7 +14,8 @@
 CLIP_LEVEL = 0.2
 EPSILON = 1e-06
 STREAMS = 4
-RIDER = 2
+RIDER = 1
+FIRST = 2
 LATE = 2
 VMEM = pl.BlockSpec(memory_space=pltpu.VMEM)
 SMEM = pl.BlockSpec(memory_space=pltpu.SMEM)
@@ -48,34 +49,41 @@
     return pltpu.CompilerParams(vmem_limit_bytes=byte_count + (1 << 20))
 
 
-def first_kernel(n, start, rows, slow_ref, fast_ref, out_ref, slow_buf, fast_buf, sems):
-    here = (chunk_index(n, 1), pl.ds(start, rows))
-    a = pltpu.make_async_copy(slow_ref.at[here], slow_buf, sems.at[0])
-    b = pltpu.make_async_copy(fast_ref.at[here], fast_buf, sems.at[1])
-    a.start()
-    b.start()
-    a.wait()
-    b.wait()
-    out_ref[...] = slow_buf[...] - fast_buf[...].astype(jnp.float32)
-
-
-def first_piece(slow, fast, n, part):
+def first_kernel(n, parts, slow_ref, fast_ref, *refs):
+    outs, (slow_buf, fast_buf, sems) = refs[: len(parts)], refs[len(parts) :]
+    index = chunk_index(n, 1)
+    copies = []
+    for s, (start, rows) in enumerate(parts):
+        here = pl.ds(start, rows)
+        a = pltpu.make_async_copy(slow_ref.at[index, here], slow_buf.at[here], sems.at[0, s])
+        b = pltpu.make_async_copy(fast_ref.at[index, here], fast_buf.at[here], sems.at[1, s])
+        a.start()
+        b.start()
+        copies.append((a, b))
+    for s, (start, rows) in enumerate(parts):
+        here = pl.ds(start, rows)
+        for copy in copies[s]:
+            copy.wait()
+        outs[s][...] = slow_buf[here] - fast_buf[here].astype(jnp.float32)
+
+
+def first_pieces(slow, fast, n, parts):
     columns = slow.shape[2]
-    rows = part[1]
+    depth = parts[-1][0] + parts[-1][1]
     slow = pltpu.with_memory_space_constraint(slow, pltpu.HBM)
     fast = pltpu.with_memory_space_constraint(fast, pltpu.HBM)
     return pl.pallas_call(
-        functools.partial(first_kernel, n, *part),
-        out_shape=jax.ShapeDtypeStruct((rows, columns), jnp.float32),
+        functools.partial(first_kernel, n, parts),
+        out_shape=[jax.ShapeDtypeStruct((rows, columns), jnp.float32) for _, rows in parts],
         in_specs=[HBM, HBM],
-        out_specs=VMEM,
+        out_specs=[VMEM] * len(parts),
         scratch_shapes=[
-            pltpu.VMEM((rows, columns), jnp.float32),
-            pltpu.VMEM((rows, columns), jnp.bfloat16),
-            pltpu.SemaphoreType.DMA((2,)),
+            pltpu.VMEM((depth, columns), jnp.float32),
+            pltpu.VMEM((depth, columns), jnp.bfloat16),
+            pltpu.SemaphoreType.DMA((2, len(parts))),
         ],
-        cost_estimate=estimate(rows * columns, 10, 1),
-        compiler_params=grant(rows * columns * 6),
+        cost_estimate=estimate(depth * columns, 10, 1),
+        compiler_params=grant(depth * columns * 6),
         name="first",
     )(slow, fast)
 
@@ -181,13 +189,46 @@
     )(piece, table, other, *state)
 
 
-def update_kernel(n, max_norm, pieces, n_outs, total_ref, slow_ref, momentum_ref, *refs):
+def unload_kernel(loaded_ref, *refs):
+    refs[-1][...] = loaded_ref[: refs[-1].shape[0], :]
+
+
+def unload_rider(loaded, rows, state):
+    return pl.pallas_call(
+        unload_kernel,
+        out_shape=jax.ShapeDtypeStruct((rows, loaded.shape[1]), jnp.float32),
+        in_specs=[VMEM] * (1 + len(state)),
+        out_specs=VMEM,
+        cost_estimate=estimate(loaded.size, 12, 1),
+        compiler_params=grant(0),
+        name="unload",
+    )(loaded, *state)
+
+
+def scale_kernel(max_norm, table_ref, *refs):
+    norm = jnp.sqrt(jnp.sum(table_ref[...], keepdims=True))
+    factor = jnp.minimum(1.0, max_norm / (norm + EPSILON))
+    refs[-1][...] = jnp.broadcast_to(factor, refs[-1].shape)
+
+
+def clip_factor(table, state, max_norm):
+    return pl.pallas_call(
+        functools.partial(scale_kernel, max_norm),
+        out_shape=jax.ShapeDtypeStruct((8, table.shape[1]), jnp.float32),
+        in_specs=[VMEM] * (1 + len(state)),
+        out_specs=VMEM,
+        cost_estimate=estimate(table.size, 12, 1),
+        compiler_params=grant(0),
+        name="scale",
+    )(table, *state)
+
+
+def update_kernel(n, pieces, n_outs, factor_ref, slow_ref, momentum_ref, *refs):
     count = len(pieces)
     sums = refs[:count]
     slow_out, momentum_out, fast_out = refs[count + n_outs : count + n_outs + 3]
     slow_buf, momentum_buf, fast_buf, sems = refs[count + n_outs + 3 :]
-    norm = jnp.sqrt(jnp.sum(total_ref[...], keepdims=True))
-    factor = jnp.minimum(1.0, max_norm / (norm + EPSILON))
+    factor = factor_ref[:1, :]
     copies = []
     at = 0
     for k, (back, start, rows) in enumerate(pieces):
@@ -210,13 +251,13 @@
         copy.wait()
 
 
-def update(total, chunks, slow, momentum, outs, n, max_norm):
+def update(factor, chunks, slow, momentum, outs, n):
     pieces = [(back, start, rows) for back, (start, rows), _ in chunks]
     count = len(chunks)
     columns = slow.shape[2]
     rows = sum(rows for _, _, rows in pieces)
     return pl.pallas_call(
-        functools.partial(update_kernel, n, max_norm, pieces, len(outs)),
+        functools.partial(update_kernel, n, pieces, len(outs)),
         out_shape=(
             pltpu.HBM(slow.shape, jnp.float32),
             pltpu.HBM(slow.shape, jnp.float32),
@@ -234,7 +275,7 @@
         cost_estimate=estimate(rows * columns, 22, 8),
         compiler_params=grant(rows * columns * 15),
         name="update",
-    )(total, slow, momentum, *[sums for _, _, sums in chunks], *outs)
+    )(factor, slow, momentum, *[sums for _, _, sums in chunks], *outs)
 
 
 def ring_order(n):
@@ -286,8 +327,8 @@
     def hop(value):
         return lax.ppermute(value, ("dp", "mp"), perm)
 
-    held = [first_piece(slow, fast, n, parts[0])]
-    held += [own_piece(slow, fast, n, part) for part in parts[1:]]
+    held = list(first_pieces(slow, fast, n, parts[:FIRST]))
+    held += [own_piece(slow, fast, n, part) for part in parts[FIRST:]]
     for step in range(n - 1):
         state = (slow, fast) if step < LATE else (slow, fast, moment)
         for s, part in enumerate(parts):
@@ -317,14 +358,17 @@
                 got[j] = swap(j, table)
         if step == n - 1:
             break
+        if riding and s == RIDER and step == 1 + n // 2:
+            held[s] = unload_rider(held[s], parts[s][1], state)
         held[s] = hop(held[s])
         if s == 0:
             chunks.append([])
         chunks[-1].append((step + 1, parts[s], held[s]))
 
+    factor = clip_factor(table, state, max_norm)
     mine = [piece for chunk in chunks[:-1] for piece in chunk]
-    outs = update(table, mine, slow, moment, (), n, max_norm)
-    outs = update(table, chunks[-1], slow, moment, outs, n, max_norm)
+    outs = update(factor, mine, slow, moment, (), n)
+    outs = update(factor, chunks[-1], slow, moment, outs, n)
     slow_next, momentum_next, fast_next = outs
     return (
         slow_next.reshape(slow_weights.shape),

time: 89.1 us -> 87 us (0.976)
  local copies, waits for them, and re-layouts: 3.55 us -> 0.01 us
    unnamed x10 -> x6, local copies, waits for them, and re-layouts: 3.55 us -> 0.01 us
    pallas_call x3 -> x5, Pallas kernels: 6.21 us -> 6.41 us  [the longest x2 5.07 us: update(): pl.pallas_call(functools.partial(update_kernel, n, pieces, len(outs)), ou...]
  transfers between devices with their start and end apart: 59 -> 59, of which waited for: 23 -> 20; matrix products, arithmetic and copies ran while one was open for 0% -> 0% of each run, Pallas kernels for 6% -> 6%
where the time goes in v2:
time: 87 us; the launch traced here: 86.8 us
  starting transfers between devices  70.4 us (81%)
  waiting for transfers between devices  8.36 us (10%)
  Pallas kernels  7.17 us (8%)
  between operations  0.88 us (1%)
    ppermute x56, starting transfers between devices, hop(): return lax.ppermute(value, ('dp', 'mp'), perm)  68.8 us
    pallas_call x2, Pallas kernels, update(): pl.pallas_call(functools.partial(update_kernel, n, pieces, len(outs)), ou...  5.07 us
    ppermute x3, waiting for transfers between devices, swap(): return lax.ppermute(value, 'mp', steps[j][0])  4.48 us
    ppermute x56, waiting for transfers between devices, hop(): return lax.ppermute(value, ('dp', 'mp'), perm)  3.88 us
  transfers between devices with their start and end apart: 59, of which 20 were waited for; matrix products, arithmetic and copies ran while one was open for 0% of the time, Pallas kernels for 6%

profile of v2, /device:TPU:0, one launch (start us, length us, event | category | flops | bytes accessed | tf_op | source)
XLA Modules:
  0.0 86.8 jit_solution(4979955938490615496)
XLA Ops:
  1.9 3.1 %collective-permute-start.7 = (f32[112,256]{1,0:T(8,128)S(1)}, f32[112,256]{1,0:T(8,128)S(1)}, u32[]{:S(2)}, u32[]{:S(2)}) collective-permute-start(f32[112,256]{1,0:T(8,128)S(1)} %get-tuple-element.12), channel_id=1, source_target_pairs={{0,8},{1,5},{2,10},{3,7},{8,16},{9,1},{10,18},{11,3},{16,24},{17,9... | collective-permute-start | bytes 344072 | tf_op jit(solution)/shard_map/ppermute | solution.py:328
  5.0 1.6 %collective-permute-start.14 = (f32[112,256]{1,0:T(8,128)S(1)}, f32[112,256]{1,0:T(8,128)S(1)}, u32[]{:S(2)}, u32[]{:S(2)}) collective-permute-start(f32[112,256]{1,0:T(8,128)S(1)} %own.2), channel_id=1, source_target_pairs={{0,8},{1,5},{2,10},{3,7},{8,16},{9,1},{10,18},{11,3},{16,24},{17,9... | collective-permute-start | bytes 344072 | tf_op jit(solution)/shard_map/ppermute | solution.py:328
  6.6 1.6 %collective-permute-start.21 = (f32[112,256]{1,0:T(8,128)S(1)}, f32[112,256]{1,0:T(8,128)S(1)}, u32[]{:S(2)}, u32[]{:S(2)}) collective-permute-start(f32[112,256]{1,0:T(8,128)S(1)} %own.3), channel_id=1, source_target_pairs={{0,8},{1,5},{2,10},{3,7},{8,16},{9,1},{10,18},{11,3},{16,24},{17,9... | collective-permute-start | bytes 344072 | tf_op jit(solution)/shard_map/ppermute | solution.py:328
  8.3 1.5 %collective-permute-start = (f32[112,256]{1,0:T(8,128)S(1)}, f32[112,256]{1,0:T(8,128)S(1)}, u32[]{:S(2)}, u32[]{:S(2)}) collective-permute-start(f32[112,256]{1,0:T(8,128)S(1)} %get-tuple-element.11), channel_id=1, source_target_pairs={{0,8},{1,5},{2,10},{3,7},{8,16},{9,1},{10,18},{11,3},{16,24},{17,9... | collective-permute-start | bytes 344072 | tf_op jit(solution)/shard_map/ppermute | solution.py:328
  9.8 1.5 %collective-permute-start.8 = (f32[112,256]{1,0:T(8,128)S(1)}, f32[112,256]{1,0:T(8,128)S(1)}, u32[]{:S(2)}, u32[]{:S(2)}) collective-permute-start(f32[112,256]{1,0:T(8,128)S(1)} %add.35), channel_id=1, source_target_pairs={{0,8},{1,5},{2,10},{3,7},{8,16},{9,1},{10,18},{11,3},{16,24},{17,9... | collective-permute-start | bytes 344072 | tf_op jit(solution)/shard_map/ppermute | solution.py:328
  11.9 1.3 %collective-permute-start.22 = (f32[112,256]{1,0:T(8,128)S(1)}, f32[112,256]{1,0:T(8,128)S(1)}, u32[]{:S(2)}, u32[]{:S(2)}) collective-permute-start(f32[112,256]{1,0:T(8,128)S(1)} %add.49), channel_id=1, source_target_pairs={{0,8},{1,5},{2,10},{3,7},{8,16},{9,1},{10,18},{11,3},{16,24},{17,9... | collective-permute-start | bytes 344072 | tf_op jit(solution)/shard_map/ppermute | solution.py:328
  13.2 1.6 %collective-permute-start.1 = (f32[112,256]{1,0:T(8,128)S(1)}, f32[112,256]{1,0:T(8,128)S(1)}, u32[]{:S(2)}, u32[]{:S(2)}) collective-permute-start(f32[112,256]{1,0:T(8,128)S(1)} %add.28), channel_id=1, source_target_pairs={{0,8},{1,5},{2,10},{3,7},{8,16},{9,1},{10,18},{11,3},{16,24},{17,9... | collective-permute-start | bytes 344072 | tf_op jit(solution)/shard_map/ppermute | solution.py:328
  14.8 1.5 %collective-permute-start.9 = (f32[112,256]{1,0:T(8,128)S(1)}, f32[112,256]{1,0:T(8,128)S(1)}, u32[]{:S(2)}, u32[]{:S(2)}) collective-permute-start(f32[112,256]{1,0:T(8,128)S(1)} %add.36), channel_id=1, source_target_pairs={{0,8},{1,5},{2,10},{3,7},{8,16},{9,1},{10,18},{11,3},{16,24},{17,9... | collective-permute-start | bytes 344072 | tf_op jit(solution)/shard_map/ppermute | solution.py:328
  16.3 1.2 %collective-permute-start.16 = (f32[112,256]{1,0:T(8,128)S(1)}, f32[112,256]{1,0:T(8,128)S(1)}, u32[]{:S(2)}, u32[]{:S(2)}) collective-permute-start(f32[112,256]{1,0:T(8,128)S(1)} %add.43), channel_id=1, source_target_pairs={{0,8},{1,5},{2,10},{3,7},{8,16},{9,1},{10,18},{11,3},{16,24},{17,9... | collective-permute-start | bytes 344072 | tf_op jit(solution)/shard_map/ppermute | solution.py:328
  17.6 1.2 %collective-permute-start.23 = (f32[112,256]{1,0:T(8,128)S(1)}, f32[112,256]{1,0:T(8,128)S(1)}, u32[]{:S(2)}, u32[]{:S(2)}) collective-permute-start(f32[112,256]{1,0:T(8,128)S(1)} %add.50), channel_id=1, source_target_pairs={{0,8},{1,5},{2,10},{3,7},{8,16},{9,1},{10,18},{11,3},{16,24},{17,9... | collective-permute-start | bytes 344072 | tf_op jit(solution)/shard_map/ppermute | solution.py:328
  18.8 1.2 %collective-permute-start.2 = (f32[112,256]{1,0:T(8,128)S(1)}, f32[112,256]{1,0:T(8,128)S(1)}, u32[]{:S(2)}, u32[]{:S(2)}) collective-permute-start(f32[112,256]{1,0:T(8,128)S(1)} %add.29), channel_id=1, source_target_pairs={{0,8},{1,5},{2,10},{3,7},{8,16},{9,1},{10,18},{11,3},{16,24},{17,9... | collective-permute-start | bytes 344072 | tf_op jit(solution)/shard_map/ppermute | solution.py:328
  21.3 1.2 %collective-permute-start.17 = (f32[112,256]{1,0:T(8,128)S(1)}, f32[112,256]{1,0:T(8,128)S(1)}, u32[]{:S(2)}, u32[]{:S(2)}) collective-permute-start(f32[112,256]{1,0:T(8,128)S(1)} %add.44), channel_id=1, source_target_pairs={{0,8},{1,5},{2,10},{3,7},{8,16},{9,1},{10,18},{11,3},{16,24},{17,9... | collective-permute-start | bytes 344072 | tf_op jit(solution)/shard_map/ppermute | solution.py:328
  26.2 1.2 %collective-permute-start.18 = (f32[112,256]{1,0:T(8,128)S(1)}, f32[112,256]{1,0:T(8,128)S(1)}, u32[]{:S(2)}, u32[]{:S(2)}) collective-permute-start(f32[112,256]{1,0:T(8,128)S(1)} %add.45), channel_id=1, source_target_pairs={{0,8},{1,5},{2,10},{3,7},{8,16},{9,1},{10,18},{11,3},{16,24},{17,9... | collective-permute-start | bytes 344072 | tf_op jit(solution)/shard_map/ppermute | solution.py:328
  28.6 1.2 %collective-permute-start.4 = (f32[112,256]{1,0:T(8,128)S(1)}, f32[112,256]{1,0:T(8,128)S(1)}, u32[]{:S(2)}, u32[]{:S(2)}) collective-permute-start(f32[112,256]{1,0:T(8,128)S(1)} %add.31), channel_id=1, source_target_pairs={{0,8},{1,5},{2,10},{3,7},{8,16},{9,1},{10,18},{11,3},{16,24},{17,9... | collective-permute-start | bytes 344072 | tf_op jit(solution)/shard_map/ppermute | solution.py:328
  33.5 1.2 %collective-permute-start.5 = (f32[112,256]{1,0:T(8,128)S(1)}, f32[112,256]{1,0:T(8,128)S(1)}, u32[]{:S(2)}, u32[]{:S(2)}) collective-permute-start(f32[112,256]{1,0:T(8,128)S(1)} %add.32), channel_id=1, source_target_pairs={{0,8},{1,5},{2,10},{3,7},{8,16},{9,1},{10,18},{11,3},{16,24},{17,9... | collective-permute-start | bytes 344072 | tf_op jit(solution)/shard_map/ppermute | solution.py:328
  36.0 1.2 %collective-permute-start.20 = (f32[112,256]{1,0:T(8,128)S(1)}, f32[112,256]{1,0:T(8,128)S(1)}, u32[]{:S(2)}, u32[]{:S(2)}) collective-permute-start(f32[112,256]{1,0:T(8,128)S(1)} %add.47), channel_id=1, source_target_pairs={{0,8},{1,5},{2,10},{3,7},{8,16},{9,1},{10,18},{11,3},{16,24},{17,9... | collective-permute-start | bytes 344072 | tf_op jit(solution)/shard_map/ppermute | solution.py:328
  38.4 1.2 %collective-permute-start.6 = (f32[112,256]{1,0:T(8,128)S(1)}, f32[112,256]{1,0:T(8,128)S(1)}, u32[]{:S(2)}, u32[]{:S(2)}) collective-permute-start(f32[112,256]{1,0:T(8,128)S(1)} %add.33), channel_id=1, source_target_pairs={{0,8},{1,5},{2,10},{3,7},{8,16},{9,1},{10,18},{11,3},{16,24},{17,9... | collective-permute-start | bytes 344072 | tf_op jit(solution)/shard_map/ppermute | solution.py:328
  40.9 1.2 %collective-permute-start.45 = (f32[112,256]{1,0:T(8,128)S(1)}, f32[112,256]{1,0:T(8,128)S(1)}, u32[]{:S(2)}, u32[]{:S(2)}) collective-permute-start(f32[112,256]{1,0:T(8,128)S(1)} %add.48.refs_2_), channel_id=1, source_target_pairs={{0,8},{1,5},{2,10},{3,7},{8,16},{9,1},{10,18},{11,3},{16,24},{17,9... | collective-permute-start | bytes 344072 | tf_op jit(solution)/shard_map/ppermute | solution.py:328
  43.4 1.2 %collective-permute-start.36 = (f32[112,256]{1,0:T(8,128)S(1)}, f32[112,256]{1,0:T(8,128)S(1)}, u32[]{:S(2)}, u32[]{:S(2)}) collective-permute-start(f32[112,256]{1,0:T(8,128)S(1)} %add.34.refs_0_), channel_id=1, source_target_pairs={{0,8},{1,5},{2,10},{3,7},{8,16},{9,1},{10,18},{11,3},{16,24},{17,9... | collective-permute-start | bytes 344072 | tf_op jit(solution)/shard_map/ppermute | solution.py:328
  65.7 1.4 %collective-permute-done.49.refs_22_ = f32[112,256]{1,0:T(8,128)S(1)} collective-permute-done((f32[112,256]{1,0:T(8,128)S(1)}, f32[112,256]{1,0:T(8,128)S(1)}, u32[]{:S(2)}, u32[]{:S(2)}) %collective-permute-start.49) | collective-permute-done | bytes 114720 | tf_op jit(solution)/shard_map/ppermute | solution.py:328
  70.7 1.2 %collective-permute-start.43 = (f32[112,256]{1,0:T(8,128)S(1)}, f32[112,256]{1,0:T(8,128)S(1)}, u32[]{:S(2)}, u32[]{:S(2)}) collective-permute-start(f32[112,256]{1,0:T(8,128)S(1)} %unload.1), channel_id=1, source_target_pairs={{0,8},{1,5},{2,10},{3,7},{8,16},{9,1},{10,18},{11,3},{16,24},{17,9... | collective-permute-start | bytes 344072 | tf_op jit(solution)/shard_map/ppermute | solution.py:328
  77.9 1.5 %collective-permute-start.35 = (f32[8,256]{1,0:T(8,128)S(1)}, f32[8,256]{1,0:T(8,128)S(1)}, u32[]{:S(2)}, u32[]{:S(2)}) collective-permute-start(f32[8,256]{1,0:T(8,128)S(1)} %merge.4.refs_0_), channel_id=1, source_target_pairs={{0,2},{1,3},{2,0},{3,1},{4,6},{5,7},{6,4},{7,5},{8,10},{9,11},{10,... | collective-permute-start | bytes 24584 | tf_op jit(solution)/shard_map/ppermute | solution.py:345
  79.4 2.2 %collective-permute-done.35.refs_1_ = f32[8,256]{1,0:T(8,128)S(1)} collective-permute-done((f32[8,256]{1,0:T(8,128)S(1)}, f32[8,256]{1,0:T(8,128)S(1)}, u32[]{:S(2)}, u32[]{:S(2)}) %collective-permute-start.35) | collective-permute-done | bytes 8224 | tf_op jit(solution)/shard_map/ppermute | solution.py:345
  81.7 3.9 %update.2 = (f32[8,448,256]{2,1,0:T(8,128)}, f32[8,448,256]{2,1,0:T(8,128)}, bf16[8,448,256]{2,1,0:T(8,128)(2,1)}) custom-call(f32[8,256]{1,0:T(8,128)S(1)} %scale.1.factor_ref, f32[8,448,256]{2,1,0:T(8,128)S(1)} %bitcast.44, f32[8,448,256]{2,1,0:T(8,128)S(1)} %bitcast.73, f32[112,256]{1,0:T(8,128)S(1)} %add.34.refs_0_, f32[112,256]{1,0:T(8,128)S(1)} %add.41.refs_1_, ...), custom_call_target="tpu_custom_call" | custom-call | flops 6422528 | bytes 17661952 | tf_op jit(solution)/shard_map/update/pallas_call | solution.py:259
  (140 shorter events, 48.8 us)
Async XLA Ops:
  1.9 7.9 %collective-permute-start.7 = (f32[112,256]{1,0:T(8,128)S(1)}, f32[112,256]{1,0:T(8,128)S(1)}, u32[]{:S(2)}, u32[]{:S(2)}) collective-permute-start(f32[112,256]{1,0:T(8,128)S(1)} %get-tuple-element.12), channel_id=1, source_target_pairs={{0,8},{1,5},{2,10},{3,7},{8,16},{9,1},{10,18},{11,3},{16,24},{17,9... | collective-permute-start | bytes 344072 | tf_op jit(solution)/shard_map/ppermute | solution.py:328
  5.0 6.4 %collective-permute-start.14 = (f32[112,256]{1,0:T(8,128)S(1)}, f32[112,256]{1,0:T(8,128)S(1)}, u32[]{:S(2)}, u32[]{:S(2)}) collective-permute-start(f32[112,256]{1,0:T(8,128)S(1)} %own.2), channel_id=1, source_target_pairs={{0,8},{1,5},{2,10},{3,7},{8,16},{9,1},{10,18},{11,3},{16,24},{17,9... | collective-permute-start | bytes 344072 | tf_op jit(solution)/shard_map/ppermute | solution.py:328
  6.6 5.2 %collective-permute-start.21 = (f32[112,256]{1,0:T(8,128)S(1)}, f32[112,256]{1,0:T(8,128)S(1)}, u32[]{:S(2)}, u32[]{:S(2)}) collective-permute-start(f32[112,256]{1,0:T(8,128)S(1)} %own.3), channel_id=1, source_target_pairs={{0,8},{1,5},{2,10},{3,7},{8,16},{9,1},{10,18},{11,3},{16,24},{17,9... | collective-permute-start | bytes 344072 | tf_op jit(solution)/shard_map/ppermute | solution.py:328
  11.9 5.6 %collective-permute-start.22 = (f32[112,256]{1,0:T(8,128)S(1)}, f32[112,256]{1,0:T(8,128)S(1)}, u32[]{:S(2)}, u32[]{:S(2)}) collective-permute-start(f32[112,256]{1,0:T(8,128)S(1)} %add.49), channel_id=1, source_target_pairs={{0,8},{1,5},{2,10},{3,7},{8,16},{9,1},{10,18},{11,3},{16,24},{17,9... | collective-permute-start | bytes 344072 | tf_op jit(solution)/shard_map/ppermute | solution.py:328
  13.2 5.6 %collective-permute-start.1 = (f32[112,256]{1,0:T(8,128)S(1)}, f32[112,256]{1,0:T(8,128)S(1)}, u32[]{:S(2)}, u32[]{:S(2)}) collective-permute-start(f32[112,256]{1,0:T(8,128)S(1)} %add.28), channel_id=1, source_target_pairs={{0,8},{1,5},{2,10},{3,7},{8,16},{9,1},{10,18},{11,3},{16,24},{17,9... | collective-permute-start | bytes 344072 | tf_op jit(solution)/shard_map/ppermute | solution.py:328
  14.8 5.2 %collective-permute-start.9 = (f32[112,256]{1,0:T(8,128)S(1)}, f32[112,256]{1,0:T(8,128)S(1)}, u32[]{:S(2)}, u32[]{:S(2)}) collective-permute-start(f32[112,256]{1,0:T(8,128)S(1)} %add.36), channel_id=1, source_target_pairs={{0,8},{1,5},{2,10},{3,7},{8,16},{9,1},{10,18},{11,3},{16,24},{17,9... | collective-permute-start | bytes 344072 | tf_op jit(solution)/shard_map/ppermute | solution.py:328
  39.7 6.2 %collective-permute-start.29 = (f32[112,256]{1,0:T(8,128)S(1)}, f32[112,256]{1,0:T(8,128)S(1)}, u32[]{:S(2)}, u32[]{:S(2)}) collective-permute-start(f32[112,256]{1,0:T(8,128)S(1)} %add.41.refs_1_), channel_id=1, source_target_pairs={{0,8},{1,5},{2,10},{3,7},{8,16},{9,1},{10,18},{11,3},{16,24},{17,9... | collective-permute-start | bytes 344072 | tf_op jit(solution)/shard_map/ppermute | solution.py:328
  40.9 6.2 %collective-permute-start.45 = (f32[112,256]{1,0:T(8,128)S(1)}, f32[112,256]{1,0:T(8,128)S(1)}, u32[]{:S(2)}, u32[]{:S(2)}) collective-permute-start(f32[112,256]{1,0:T(8,128)S(1)} %add.48.refs_2_), channel_id=1, source_target_pairs={{0,8},{1,5},{2,10},{3,7},{8,16},{9,1},{10,18},{11,3},{16,24},{17,9... | collective-permute-start | bytes 344072 | tf_op jit(solution)/shard_map/ppermute | solution.py:328
  42.1 6.1 %collective-permute-start.52 = (f32[112,256]{1,0:T(8,128)S(1)}, f32[112,256]{1,0:T(8,128)S(1)}, u32[]{:S(2)}, u32[]{:S(2)}) collective-permute-start(f32[112,256]{1,0:T(8,128)S(1)} %add.55.refs_3_), channel_id=1, source_target_pairs={{0,8},{1,5},{2,10},{3,7},{8,16},{9,1},{10,18},{11,3},{16,24},{17,9... | collective-permute-start | bytes 344072 | tf_op jit(solution)/shard_map/ppermute | solution.py:328
  43.4 6.1 %collective-permute-start.36 = (f32[112,256]{1,0:T(8,128)S(1)}, f32[112,256]{1,0:T(8,128)S(1)}, u32[]{:S(2)}, u32[]{:S(2)}) collective-permute-start(f32[112,256]{1,0:T(8,128)S(1)} %add.34.refs_0_), channel_id=1, source_target_pairs={{0,8},{1,5},{2,10},{3,7},{8,16},{9,1},{10,18},{11,3},{16,24},{17,9... | collective-permute-start | bytes 344072 | tf_op jit(solution)/shard_map/ppermute | solution.py:328
  48.3 5.0 %collective-permute-start.53 = (f32[112,256]{1,0:T(8,128)S(1)}, f32[112,256]{1,0:T(8,128)S(1)}, u32[]{:S(2)}, u32[]{:S(2)}) collective-permute-start(f32[112,256]{1,0:T(8,128)S(1)} %collective-permute-done.52.refs_7_), channel_id=1, source_target_pairs={{0,8},{1,5},{2,10},{3,7},{8,16},{9,1},{10,18},{11,3},{16,24},{17,9... | collective-permute-start | bytes 344072 | tf_op jit(solution)/shard_map/ppermute | solution.py:328
  49.4 5.1 %collective-permute-start.37 = (f32[112,256]{1,0:T(8,128)S(1)}, f32[112,256]{1,0:T(8,128)S(1)}, u32[]{:S(2)}, u32[]{:S(2)}) collective-permute-start(f32[112,256]{1,0:T(8,128)S(1)} %collective-permute-done.36.refs_4_), channel_id=1, source_target_pairs={{0,8},{1,5},{2,10},{3,7},{8,16},{9,1},{10,18},{11,3},{16,24},{17,9... | collective-permute-start | bytes 344072 | tf_op jit(solution)/shard_map/ppermute | solution.py:328
  52.1 5.0 %collective-permute-start.47 = (f32[112,256]{1,0:T(8,128)S(1)}, f32[112,256]{1,0:T(8,128)S(1)}, u32[]{:S(2)}, u32[]{:S(2)}) collective-permute-start(f32[112,256]{1,0:T(8,128)S(1)} %collective-permute-done.46.refs_10_), channel_id=1, source_target_pairs={{0,8},{1,5},{2,10},{3,7},{8,16},{9,1},{10,18},{11,3},{16,24},{17,9... | collective-permute-start | bytes 344072 | tf_op jit(solution)/shard_map/ppermute | solution.py:328
  53.3 5.0 %collective-permute-start.54 = (f32[112,256]{1,0:T(8,128)S(1)}, f32[112,256]{1,0:T(8,128)S(1)}, u32[]{:S(2)}, u32[]{:S(2)}) collective-permute-start(f32[112,256]{1,0:T(8,128)S(1)} %collective-permute-done.53.refs_11_), channel_id=1, source_target_pairs={{0,8},{1,5},{2,10},{3,7},{8,16},{9,1},{10,18},{11,3},{16,24},{17,9... | collective-permute-start | bytes 344072 | tf_op jit(solution)/shard_map/ppermute | solution.py:328
  55.8 5.0 %collective-permute-start.32 = (f32[120,256]{1,0:T(8,128)S(1)}, f32[120,256]{1,0:T(8,128)S(1)}, u32[]{:S(2)}, u32[]{:S(2)}) collective-permute-start(f32[120,256]{1,0:T(8,128)S(1)} %collective-permute-done.31.refs_3_.refs_13_), channel_id=1, source_target_pairs={{0,8},{1,5},{2,10},{3,7},{8,16},{9,1},{10,18},{11,3},{16,24},{17,9... | collective-permute-start | bytes 368648 | tf_op jit(solution)/shard_map/ppermute | solution.py:328
  57.1 5.0 %collective-permute-start.48 = (f32[112,256]{1,0:T(8,128)S(1)}, f32[112,256]{1,0:T(8,128)S(1)}, u32[]{:S(2)}, u32[]{:S(2)}) collective-permute-start(f32[112,256]{1,0:T(8,128)S(1)} %collective-permute-done.47.refs_14_), channel_id=1, source_target_pairs={{0,8},{1,5},{2,10},{3,7},{8,16},{9,1},{10,18},{11,3},{16,24},{17,9... | collective-permute-start | bytes 344072 | tf_op jit(solution)/shard_map/ppermute | solution.py:328
  58.3 5.0 %collective-permute-start.55 = (f32[112,256]{1,0:T(8,128)S(1)}, f32[112,256]{1,0:T(8,128)S(1)}, u32[]{:S(2)}, u32[]{:S(2)}) collective-permute-start(f32[112,256]{1,0:T(8,128)S(1)} %collective-permute-done.54.refs_15_), channel_id=1, source_target_pairs={{0,8},{1,5},{2,10},{3,7},{8,16},{9,1},{10,18},{11,3},{16,24},{17,9... | collective-permute-start | bytes 344072 | tf_op jit(solution)/shard_map/ppermute | solution.py:328
  60.8 9.8 %collective-permute-start.33 = (f32[120,256]{1,0:T(8,128)S(1)}, f32[120,256]{1,0:T(8,128)S(1)}, u32[]{:S(2)}, u32[]{:S(2)}) collective-permute-start(f32[120,256]{1,0:T(8,128)S(1)} %collective-permute-done.32.refs_4_.refs_17_), channel_id=1, source_target_pairs={{0,8},{1,5},{2,10},{3,7},{8,16},{9,1},{10,18},{11,3},{16,24},{17,9... | collective-permute-start | bytes 368648 | tf_op jit(solution)/shard_map/ppermute | solution.py:328
  62.1 5.0 %collective-permute-start.49 = (f32[112,256]{1,0:T(8,128)S(1)}, f32[112,256]{1,0:T(8,128)S(1)}, u32[]{:S(2)}, u32[]{:S(2)}) collective-permute-start(f32[112,256]{1,0:T(8,128)S(1)} %collective-permute-done.48.refs_18_), channel_id=1, source_target_pairs={{0,8},{1,5},{2,10},{3,7},{8,16},{9,1},{10,18},{11,3},{16,24},{17,9... | collective-permute-start | bytes 344072 | tf_op jit(solution)/shard_map/ppermute | solution.py:328
  63.3 5.0 %collective-permute-start.56 = (f32[112,256]{1,0:T(8,128)S(1)}, f32[112,256]{1,0:T(8,128)S(1)}, u32[]{:S(2)}, u32[]{:S(2)}) collective-permute-start(f32[112,256]{1,0:T(8,128)S(1)} %collective-permute-done.55.refs_19_), channel_id=1, source_target_pairs={{0,8},{1,5},{2,10},{3,7},{8,16},{9,1},{10,18},{11,3},{16,24},{17,9... | collective-permute-start | bytes 344072 | tf_op jit(solution)/shard_map/ppermute | solution.py:328
  71.9 13.7 %collective-permute-start.51 = (f32[112,256]{1,0:T(8,128)S(1)}, f32[112,256]{1,0:T(8,128)S(1)}, u32[]{:S(2)}, u32[]{:S(2)}) collective-permute-start(f32[112,256]{1,0:T(8,128)S(1)} %collective-permute-done.50.refs_26_), channel_id=1, source_target_pairs={{0,8},{1,5},{2,10},{3,7},{8,16},{9,1},{10,18},{11,3},{16,24},{17,9... | collective-permute-start | bytes 344072 | tf_op jit(solution)/shard_map/ppermute | solution.py:328
  73.1 12.5 %collective-permute-start.58 = (f32[112,256]{1,0:T(8,128)S(1)}, f32[112,256]{1,0:T(8,128)S(1)}, u32[]{:S(2)}, u32[]{:S(2)}) collective-permute-start(f32[112,256]{1,0:T(8,128)S(1)} %collective-permute-done.57.refs_27_), channel_id=1, source_target_pairs={{0,8},{1,5},{2,10},{3,7},{8,16},{9,1},{10,18},{11,3},{16,24},{17,9... | collective-permute-start | bytes 344072 | tf_op jit(solution)/shard_map/ppermute | solution.py:328
  74.3 11.3 %collective-permute-start.42 = (f32[112,256]{1,0:T(8,128)S(1)}, f32[112,256]{1,0:T(8,128)S(1)}, u32[]{:S(2)}, u32[]{:S(2)}) collective-permute-start(f32[112,256]{1,0:T(8,128)S(1)} %collective-permute-done.41.refs_24_), channel_id=1, source_target_pairs={{0,8},{1,5},{2,10},{3,7},{8,16},{9,1},{10,18},{11,3},{16,24},{17,9... | collective-permute-start | bytes 344072 | tf_op jit(solution)/shard_map/ppermute | solution.py:328
  75.6 10.1 %collective-permute-start.44 = (f32[112,256]{1,0:T(8,128)S(1)}, f32[112,256]{1,0:T(8,128)S(1)}, u32[]{:S(2)}, u32[]{:S(2)}) collective-permute-start(f32[112,256]{1,0:T(8,128)S(1)} %collective-permute-done.43.refs_25_), channel_id=1, source_target_pairs={{0,8},{1,5},{2,10},{3,7},{8,16},{9,1},{10,18},{11,3},{16,24},{17,9... | collective-permute-start | bytes 344072 | tf_op jit(solution)/shard_map/ppermute | solution.py:328
  (38 other events, 174.0 us)

commit v3 on v2

--- a/solution.py
+++ b/solution.py
@@ -244,7 +244,7 @@
             ((slow_buf, slow_out), (momentum_buf, momentum_out), (fast_buf, fast_out))
         ):
             copy = pltpu.make_async_copy(buf.at[there], out.at[index, here], sems.at[j, k])
-            copy.start()
+            copy.start(priority=j % 2)
             copies.append(copy)
         at += rows
     for copy in copies:
@@ -284,12 +284,12 @@
     return [2 * k for k in range(n // 2)] + [n - 1 - 2 * k for k in range(n // 2)]
 
 
-def ring_perm(n, m):
+def ring_perm(n, m, back=False):
     order = ring_order(n)
     perm = []
     for k in range(n):
         for c in range(m):
-            other = (k + 1) % n if c % 2 == 0 else (k - 1) % n
+            other = (k + 1) % n if (c % 2 == 0) != back else (k - 1) % n
             perm.append((order[k] * m + c, order[other] * m + c))
     return perm
 
@@ -299,7 +299,7 @@
 
 
 def exchanges(n, m):
-    hops = STREAMS * (n - 1)
+    hops = STREAMS * (n - 1) - 1
     arrived = STREAMS * (1 + n // 2) + RIDER
     swap = [(c, c ^ 1) for c in range(m)]
     steps = [(swap, STREAMS, STREAMS + RIDER), (swap, arrived + 1, arrived + 3)]
@@ -311,6 +311,10 @@
     return steps
 
 
+def back_slot(n, m):
+    return exchanges(n, m)[-1][1] if rides(n, m) else STREAMS * (n - 1) - 2
+
+
 def body(slow_weights, fast_weights, momentum):
     n, m = lax.axis_size("dp"), lax.axis_size("mp")
     rows, columns = slow_weights.shape[1:]
@@ -320,12 +324,12 @@
     fast = fast_weights.reshape(n, depth, columns)
     moment = momentum.reshape(n, depth, columns)
     parts = split(depth)
-    perm = ring_perm(n, m)
+    perm, back_perm = ring_perm(n, m), ring_perm(n, m, back=True)
     riding = rides(n, m)
     steps = exchanges(n, m) if riding else []
 
-    def hop(value):
-        return lax.ppermute(value, ("dp", "mp"), perm)
+    def hop(value, pairs=perm):
+        return lax.ppermute(value, ("dp", "mp"), pairs)
 
     held = list(first_pieces(slow, fast, n, parts[:FIRST]))
     held += [own_piece(slow, fast, n, part) for part in parts[FIRST:]]
@@ -344,8 +348,11 @@
     def swap(j, value):
         return lax.ppermute(value, "mp", steps[j][0])
 
-    for slot in range(STREAMS * (n - 1) + 1):
+    hops = STREAMS * (n - 1) - 1
+    for slot in range(hops + 1):
         step, s = divmod(slot, STREAMS)
+        if slot == back_slot(n, m):
+            final = hop(chunks[0][-1][2], back_perm)
         for j, (_, start, end) in enumerate(steps):
             if slot == end and j == 0:
                 held[s] = load_rider(held[s], table, got[j], state)
@@ -356,7 +363,7 @@
                     riders = [chunk[RIDER][2] for chunk in chunks[2 : 2 + n // 2]]
                     table = merge([table, got[0]] + riders, state, "max")
                 got[j] = swap(j, table)
-        if step == n - 1:
+        if slot == hops:
             break
         if riding and s == RIDER and step == 1 + n // 2:
             held[s] = unload_rider(held[s], parts[s][1], state)
@@ -365,6 +372,7 @@
             chunks.append([])
         chunks[-1].append((step + 1, parts[s], held[s]))
 
+    chunks[0].append((n - 1, parts[-1], final))
     factor = clip_factor(table, state, max_norm)
     mine = [piece for chunk in chunks[:-1] for piece in chunk]
     outs = update(factor, mine, slow, moment, (), n)

time: 87 us -> 85.6 us (0.984)
    ppermute x3, waiting for transfers between devices: 4.48 us -> 3.6 us  [swap(): return lax.ppermute(value, 'mp', steps[j][0])]
  transfers between devices with their start and end apart: 59 -> 59, of which waited for: 20 -> 19; matrix products, arithmetic and copies ran while one was open for 0% -> 0% of each run, Pallas kernels for 6% -> 6%
where the time goes in v3:
time: 85.6 us; the launch traced here: 85.4 us
  starting transfers between devices  69.7 us (81%)
  waiting for transfers between devices  7.72 us (9%)
  Pallas kernels  7.19 us (8%)
    ppermute x56, starting transfers between devices, hop(): return lax.ppermute(value, ('dp', 'mp'), pairs)  68.1 us
    pallas_call x2, Pallas kernels, update(): pl.pallas_call(functools.partial(update_kernel, n, pieces, len(outs)), ou...  5.06 us
    ppermute x56, waiting for transfers between devices, hop(): return lax.ppermute(value, ('dp', 'mp'), pairs)  4.12 us
    ppermute x3, waiting for transfers between devices, swap(): return lax.ppermute(value, 'mp', steps[j][0])  3.6 us
  transfers between devices with their start and end apart: 59, of which 19 were waited for; matrix products, arithmetic and copies ran while one was open for 0% of the time, Pallas kernels for 6%

profile of v3, /device:TPU:0, one launch (start us, length us, event | category | flops | bytes accessed | tf_op | source)
XLA Modules:
  0.0 85.4 jit_solution(14427281063831184340)
XLA Ops:
  1.9 3.1 %collective-permute-start.7 = (f32[112,256]{1,0:T(8,128)S(1)}, f32[112,256]{1,0:T(8,128)S(1)}, u32[]{:S(2)}, u32[]{:S(2)}) collective-permute-start(f32[112,256]{1,0:T(8,128)S(1)} %get-tuple-element.12), channel_id=1, source_target_pairs={{0,8},{1,5},{2,10},{3,7},{8,16},{9,1},{10,18},{11,3},{16,24},{17,9... | collective-permute-start | bytes 344072 | tf_op jit(solution)/shard_map/ppermute | solution.py:332
  5.0 1.6 %collective-permute-start.14 = (f32[112,256]{1,0:T(8,128)S(1)}, f32[112,256]{1,0:T(8,128)S(1)}, u32[]{:S(2)}, u32[]{:S(2)}) collective-permute-start(f32[112,256]{1,0:T(8,128)S(1)} %own.2), channel_id=1, source_target_pairs={{0,8},{1,5},{2,10},{3,7},{8,16},{9,1},{10,18},{11,3},{16,24},{17,9... | collective-permute-start | bytes 344072 | tf_op jit(solution)/shard_map/ppermute | solution.py:332
  6.6 1.6 %collective-permute-start = (f32[112,256]{1,0:T(8,128)S(1)}, f32[112,256]{1,0:T(8,128)S(1)}, u32[]{:S(2)}, u32[]{:S(2)}) collective-permute-start(f32[112,256]{1,0:T(8,128)S(1)} %get-tuple-element.11), channel_id=1, source_target_pairs={{0,8},{1,5},{2,10},{3,7},{8,16},{9,1},{10,18},{11,3},{16,24},{17,9... | collective-permute-start | bytes 344072 | tf_op jit(solution)/shard_map/ppermute | solution.py:332
  8.2 1.6 %collective-permute-start.21 = (f32[112,256]{1,0:T(8,128)S(1)}, f32[112,256]{1,0:T(8,128)S(1)}, u32[]{:S(2)}, u32[]{:S(2)}) collective-permute-start(f32[112,256]{1,0:T(8,128)S(1)} %own.3), channel_id=1, source_target_pairs={{0,8},{1,5},{2,10},{3,7},{8,16},{9,1},{10,18},{11,3},{16,24},{17,9... | collective-permute-start | bytes 344072 | tf_op jit(solution)/shard_map/ppermute | solution.py:332
  9.8 1.5 %collective-permute-start.8 = (f32[112,256]{1,0:T(8,128)S(1)}, f32[112,256]{1,0:T(8,128)S(1)}, u32[]{:S(2)}, u32[]{:S(2)}) collective-permute-start(f32[112,256]{1,0:T(8,128)S(1)} %add.35), channel_id=1, source_target_pairs={{0,8},{1,5},{2,10},{3,7},{8,16},{9,1},{10,18},{11,3},{16,24},{17,9... | collective-permute-start | bytes 344072 | tf_op jit(solution)/shard_map/ppermute | solution.py:332
  11.9 1.3 %collective-permute-start.1 = (f32[112,256]{1,0:T(8,128)S(1)}, f32[112,256]{1,0:T(8,128)S(1)}, u32[]{:S(2)}, u32[]{:S(2)}) collective-permute-start(f32[112,256]{1,0:T(8,128)S(1)} %add.28), channel_id=1, source_target_pairs={{0,8},{1,5},{2,10},{3,7},{8,16},{9,1},{10,18},{11,3},{16,24},{17,9... | collective-permute-start | bytes 344072 | tf_op jit(solution)/shard_map/ppermute | solution.py:332
  13.2 1.6 %collective-permute-start.22 = (f32[112,256]{1,0:T(8,128)S(1)}, f32[112,256]{1,0:T(8,128)S(1)}, u32[]{:S(2)}, u32[]{:S(2)}) collective-permute-start(f32[112,256]{1,0:T(8,128)S(1)} %add.49), channel_id=1, source_target_pairs={{0,8},{1,5},{2,10},{3,7},{8,16},{9,1},{10,18},{11,3},{16,24},{17,9... | collective-permute-start | bytes 344072 | tf_op jit(solution)/shard_map/ppermute | solution.py:332
  14.8 1.5 %collective-permute-start.9 = (f32[112,256]{1,0:T(8,128)S(1)}, f32[112,256]{1,0:T(8,128)S(1)}, u32[]{:S(2)}, u32[]{:S(2)}) collective-permute-start(f32[112,256]{1,0:T(8,128)S(1)} %add.36), channel_id=1, source_target_pairs={{0,8},{1,5},{2,10},{3,7},{8,16},{9,1},{10,18},{11,3},{16,24},{17,9... | collective-permute-start | bytes 344072 | tf_op jit(solution)/shard_map/ppermute | solution.py:332
  16.3 1.2 %collective-permute-start.16 = (f32[112,256]{1,0:T(8,128)S(1)}, f32[112,256]{1,0:T(8,128)S(1)}, u32[]{:S(2)}, u32[]{:S(2)}) collective-permute-start(f32[112,256]{1,0:T(8,128)S(1)} %add.43), channel_id=1, source_target_pairs={{0,8},{1,5},{2,10},{3,7},{8,16},{9,1},{10,18},{11,3},{16,24},{17,9... | collective-permute-start | bytes 344072 | tf_op jit(solution)/shard_map/ppermute | solution.py:332
  17.6 1.2 %collective-permute-start.2 = (f32[112,256]{1,0:T(8,128)S(1)}, f32[112,256]{1,0:T(8,128)S(1)}, u32[]{:S(2)}, u32[]{:S(2)}) collective-permute-start(f32[112,256]{1,0:T(8,128)S(1)} %add.29), channel_id=1, source_target_pairs={{0,8},{1,5},{2,10},{3,7},{8,16},{9,1},{10,18},{11,3},{16,24},{17,9... | collective-permute-start | bytes 344072 | tf_op jit(solution)/shard_map/ppermute | solution.py:332
  18.8 1.2 %collective-permute-start.23 = (f32[112,256]{1,0:T(8,128)S(1)}, f32[112,256]{1,0:T(8,128)S(1)}, u32[]{:S(2)}, u32[]{:S(2)}) collective-permute-start(f32[112,256]{1,0:T(8,128)S(1)} %add.50), channel_id=1, source_target_pairs={{0,8},{1,5},{2,10},{3,7},{8,16},{9,1},{10,18},{11,3},{16,24},{17,9... | collective-permute-start | bytes 344072 | tf_op jit(solution)/shard_map/ppermute | solution.py:332
  21.3 1.2 %collective-permute-start.17 = (f32[112,256]{1,0:T(8,128)S(1)}, f32[112,256]{1,0:T(8,128)S(1)}, u32[]{:S(2)}, u32[]{:S(2)}) collective-permute-start(f32[112,256]{1,0:T(8,128)S(1)} %add.44), channel_id=1, source_target_pairs={{0,8},{1,5},{2,10},{3,7},{8,16},{9,1},{10,18},{11,3},{16,24},{17,9... | collective-permute-start | bytes 344072 | tf_op jit(solution)/shard_map/ppermute | solution.py:332
  26.2 1.2 %collective-permute-start.18 = (f32[112,256]{1,0:T(8,128)S(1)}, f32[112,256]{1,0:T(8,128)S(1)}, u32[]{:S(2)}, u32[]{:S(2)}) collective-permute-start(f32[112,256]{1,0:T(8,128)S(1)} %add.45), channel_id=1, source_target_pairs={{0,8},{1,5},{2,10},{3,7},{8,16},{9,1},{10,18},{11,3},{16,24},{17,9... | collective-permute-start | bytes 344072 | tf_op jit(solution)/shard_map/ppermute | solution.py:332
  27.4 1.2 %collective-permute-start.4 = (f32[112,256]{1,0:T(8,128)S(1)}, f32[112,256]{1,0:T(8,128)S(1)}, u32[]{:S(2)}, u32[]{:S(2)}) collective-permute-start(f32[112,256]{1,0:T(8,128)S(1)} %add.31), channel_id=1, source_target_pairs={{0,8},{1,5},{2,10},{3,7},{8,16},{9,1},{10,18},{11,3},{16,24},{17,9... | collective-permute-start | bytes 344072 | tf_op jit(solution)/shard_map/ppermute | solution.py:332
  31.1 1.2 %collective-permute-start.19 = (f32[112,256]{1,0:T(8,128)S(1)}, f32[112,256]{1,0:T(8,128)S(1)}, u32[]{:S(2)}, u32[]{:S(2)}) collective-permute-start(f32[112,256]{1,0:T(8,128)S(1)} %add.46), channel_id=1, source_target_pairs={{0,8},{1,5},{2,10},{3,7},{8,16},{9,1},{10,18},{11,3},{16,24},{17,9... | collective-permute-start | bytes 344072 | tf_op jit(solution)/shard_map/ppermute | solution.py:332
  32.3 1.2 %collective-permute-start.5 = (f32[112,256]{1,0:T(8,128)S(1)}, f32[112,256]{1,0:T(8,128)S(1)}, u32[]{:S(2)}, u32[]{:S(2)}) collective-permute-start(f32[112,256]{1,0:T(8,128)S(1)} %add.32), channel_id=1, source_target_pairs={{0,8},{1,5},{2,10},{3,7},{8,16},{9,1},{10,18},{11,3},{16,24},{17,9... | collective-permute-start | bytes 344072 | tf_op jit(solution)/shard_map/ppermute | solution.py:332
  36.0 1.2 %collective-permute-start.20 = (f32[112,256]{1,0:T(8,128)S(1)}, f32[112,256]{1,0:T(8,128)S(1)}, u32[]{:S(2)}, u32[]{:S(2)}) collective-permute-start(f32[112,256]{1,0:T(8,128)S(1)} %add.47), channel_id=1, source_target_pairs={{0,8},{1,5},{2,10},{3,7},{8,16},{9,1},{10,18},{11,3},{16,24},{17,9... | collective-permute-start | bytes 344072 | tf_op jit(solution)/shard_map/ppermute | solution.py:332
  37.2 1.2 %collective-permute-start.6 = (f32[112,256]{1,0:T(8,128)S(1)}, f32[112,256]{1,0:T(8,128)S(1)}, u32[]{:S(2)}, u32[]{:S(2)}) collective-permute-start(f32[112,256]{1,0:T(8,128)S(1)} %add.33), channel_id=1, source_target_pairs={{0,8},{1,5},{2,10},{3,7},{8,16},{9,1},{10,18},{11,3},{16,24},{17,9... | collective-permute-start | bytes 344072 | tf_op jit(solution)/shard_map/ppermute | solution.py:332
  40.9 1.2 %collective-permute-start.45 = (f32[112,256]{1,0:T(8,128)S(1)}, f32[112,256]{1,0:T(8,128)S(1)}, u32[]{:S(2)}, u32[]{:S(2)}) collective-permute-start(f32[112,256]{1,0:T(8,128)S(1)} %add.48.refs_2_), channel_id=1, source_target_pairs={{0,8},{1,5},{2,10},{3,7},{8,16},{9,1},{10,18},{11,3},{16,24},{17,9... | collective-permute-start | bytes 344072 | tf_op jit(solution)/shard_map/ppermute | solution.py:332
  42.1 1.2 %collective-permute-start.36 = (f32[112,256]{1,0:T(8,128)S(1)}, f32[112,256]{1,0:T(8,128)S(1)}, u32[]{:S(2)}, u32[]{:S(2)}) collective-permute-start(f32[112,256]{1,0:T(8,128)S(1)} %add.34.refs_0_), channel_id=1, source_target_pairs={{0,8},{1,5},{2,10},{3,7},{8,16},{9,1},{10,18},{11,3},{16,24},{17,9... | collective-permute-start | bytes 344072 | tf_op jit(solution)/shard_map/ppermute | solution.py:332
  64.5 1.4 %collective-permute-done.56.refs_20_ = f32[112,256]{1,0:T(8,128)S(1)} collective-permute-done((f32[112,256]{1,0:T(8,128)S(1)}, f32[112,256]{1,0:T(8,128)S(1)}, u32[]{:S(2)}, u32[]{:S(2)}) %collective-permute-start.56) | collective-permute-done | bytes 114720 | tf_op jit(solution)/shard_map/ppermute | solution.py:332
  71.9 1.5 %collective-permute-start.35 = (f32[8,256]{1,0:T(8,128)S(1)}, f32[8,256]{1,0:T(8,128)S(1)}, u32[]{:S(2)}, u32[]{:S(2)}) collective-permute-start(f32[8,256]{1,0:T(8,128)S(1)} %merge.4.refs_0_), channel_id=1, source_target_pairs={{0,2},{1,3},{2,0},{3,1},{4,6},{5,7},{6,4},{7,5},{8,10},{9,11},{10,... | collective-permute-start | bytes 24584 | tf_op jit(solution)/shard_map/ppermute | solution.py:349
  74.3 1.3 %collective-permute-done.35.refs_1_ = f32[8,256]{1,0:T(8,128)S(1)} collective-permute-done((f32[8,256]{1,0:T(8,128)S(1)}, f32[8,256]{1,0:T(8,128)S(1)}, u32[]{:S(2)}, u32[]{:S(2)}) %collective-permute-start.35) | collective-permute-done | bytes 8224 | tf_op jit(solution)/shard_map/ppermute | solution.py:349
  80.3 4.0 %update.2 = (f32[8,448,256]{2,1,0:T(8,128)}, f32[8,448,256]{2,1,0:T(8,128)}, bf16[8,448,256]{2,1,0:T(8,128)(2,1)}) custom-call(f32[8,256]{1,0:T(8,128)S(1)} %scale.1.factor_ref, f32[8,448,256]{2,1,0:T(8,128)S(1)} %bitcast.44, f32[8,448,256]{2,1,0:T(8,128)S(1)} %bitcast.73, f32[112,256]{1,0:T(8,128)S(1)} %add.34.refs_0_, f32[112,256]{1,0:T(8,128)S(1)} %add.41.refs_1_, ...), custom_call_target="tpu_custom_call" | custom-call | flops 6651904 | bytes 18292736 | tf_op jit(solution)/shard_map/update/pallas_call | solution.py:259
  (140 shorter events, 48.2 us)
Async XLA Ops:
  1.9 7.9 %collective-permute-start.7 = (f32[112,256]{1,0:T(8,128)S(1)}, f32[112,256]{1,0:T(8,128)S(1)}, u32[]{:S(2)}, u32[]{:S(2)}) collective-permute-start(f32[112,256]{1,0:T(8,128)S(1)} %get-tuple-element.12), channel_id=1, source_target_pairs={{0,8},{1,5},{2,10},{3,7},{8,16},{9,1},{10,18},{11,3},{16,24},{17,9... | collective-permute-start | bytes 344072 | tf_op jit(solution)/shard_map/ppermute | solution.py:332
  5.0 6.4 %collective-permute-start.14 = (f32[112,256]{1,0:T(8,128)S(1)}, f32[112,256]{1,0:T(8,128)S(1)}, u32[]{:S(2)}, u32[]{:S(2)}) collective-permute-start(f32[112,256]{1,0:T(8,128)S(1)} %own.2), channel_id=1, source_target_pairs={{0,8},{1,5},{2,10},{3,7},{8,16},{9,1},{10,18},{11,3},{16,24},{17,9... | collective-permute-start | bytes 344072 | tf_op jit(solution)/shard_map/ppermute | solution.py:332
  6.6 5.3 %collective-permute-start = (f32[112,256]{1,0:T(8,128)S(1)}, f32[112,256]{1,0:T(8,128)S(1)}, u32[]{:S(2)}, u32[]{:S(2)}) collective-permute-start(f32[112,256]{1,0:T(8,128)S(1)} %get-tuple-element.11), channel_id=1, source_target_pairs={{0,8},{1,5},{2,10},{3,7},{8,16},{9,1},{10,18},{11,3},{16,24},{17,9... | collective-permute-start | bytes 344072 | tf_op jit(solution)/shard_map/ppermute | solution.py:332
  11.9 5.6 %collective-permute-start.1 = (f32[112,256]{1,0:T(8,128)S(1)}, f32[112,256]{1,0:T(8,128)S(1)}, u32[]{:S(2)}, u32[]{:S(2)}) collective-permute-start(f32[112,256]{1,0:T(8,128)S(1)} %add.28), channel_id=1, source_target_pairs={{0,8},{1,5},{2,10},{3,7},{8,16},{9,1},{10,18},{11,3},{16,24},{17,9... | collective-permute-start | bytes 344072 | tf_op jit(solution)/shard_map/ppermute | solution.py:332
  13.2 5.6 %collective-permute-start.22 = (f32[112,256]{1,0:T(8,128)S(1)}, f32[112,256]{1,0:T(8,128)S(1)}, u32[]{:S(2)}, u32[]{:S(2)}) collective-permute-start(f32[112,256]{1,0:T(8,128)S(1)} %add.49), channel_id=1, source_target_pairs={{0,8},{1,5},{2,10},{3,7},{8,16},{9,1},{10,18},{11,3},{16,24},{17,9... | collective-permute-start | bytes 344072 | tf_op jit(solution)/shard_map/ppermute | solution.py:332
  14.8 5.2 %collective-permute-start.9 = (f32[112,256]{1,0:T(8,128)S(1)}, f32[112,256]{1,0:T(8,128)S(1)}, u32[]{:S(2)}, u32[]{:S(2)}) collective-permute-start(f32[112,256]{1,0:T(8,128)S(1)} %add.36), channel_id=1, source_target_pairs={{0,8},{1,5},{2,10},{3,7},{8,16},{9,1},{10,18},{11,3},{16,24},{17,9... | collective-permute-start | bytes 344072 | tf_op jit(solution)/shard_map/ppermute | solution.py:332
  39.7 5.0 %collective-permute-start.29 = (f32[112,256]{1,0:T(8,128)S(1)}, f32[112,256]{1,0:T(8,128)S(1)}, u32[]{:S(2)}, u32[]{:S(2)}) collective-permute-start(f32[112,256]{1,0:T(8,128)S(1)} %add.41.refs_1_), channel_id=1, source_target_pairs={{0,8},{1,5},{2,10},{3,7},{8,16},{9,1},{10,18},{11,3},{16,24},{17,9... | collective-permute-start | bytes 344072 | tf_op jit(solution)/shard_map/ppermute | solution.py:332
  40.9 6.2 %collective-permute-start.45 = (f32[112,256]{1,0:T(8,128)S(1)}, f32[112,256]{1,0:T(8,128)S(1)}, u32[]{:S(2)}, u32[]{:S(2)}) collective-permute-start(f32[112,256]{1,0:T(8,128)S(1)} %add.48.refs_2_), channel_id=1, source_target_pairs={{0,8},{1,5},{2,10},{3,7},{8,16},{9,1},{10,18},{11,3},{16,24},{17,9... | collective-permute-start | bytes 344072 | tf_op jit(solution)/shard_map/ppermute | solution.py:332
  42.1 6.1 %collective-permute-start.36 = (f32[112,256]{1,0:T(8,128)S(1)}, f32[112,256]{1,0:T(8,128)S(1)}, u32[]{:S(2)}, u32[]{:S(2)}) collective-permute-start(f32[112,256]{1,0:T(8,128)S(1)} %add.34.refs_0_), channel_id=1, source_target_pairs={{0,8},{1,5},{2,10},{3,7},{8,16},{9,1},{10,18},{11,3},{16,24},{17,9... | collective-permute-start | bytes 344072 | tf_op jit(solution)/shard_map/ppermute | solution.py:332
  47.1 5.0 %collective-permute-start.46 = (f32[112,256]{1,0:T(8,128)S(1)}, f32[112,256]{1,0:T(8,128)S(1)}, u32[]{:S(2)}, u32[]{:S(2)}) collective-permute-start(f32[112,256]{1,0:T(8,128)S(1)} %collective-permute-done.45.refs_7_), channel_id=1, source_target_pairs={{0,8},{1,5},{2,10},{3,7},{8,16},{9,1},{10,18},{11,3},{16,24},{17,9... | collective-permute-start | bytes 344072 | tf_op jit(solution)/shard_map/ppermute | solution.py:332
  48.2 5.1 %collective-permute-start.37 = (f32[112,256]{1,0:T(8,128)S(1)}, f32[112,256]{1,0:T(8,128)S(1)}, u32[]{:S(2)}, u32[]{:S(2)}) collective-permute-start(f32[112,256]{1,0:T(8,128)S(1)} %collective-permute-done.36.refs_5_), channel_id=1, source_target_pairs={{0,8},{1,5},{2,10},{3,7},{8,16},{9,1},{10,18},{11,3},{16,24},{17,9... | collective-permute-start | bytes 344072 | tf_op jit(solution)/shard_map/ppermute | solution.py:332
  49.6 5.0 %collective-permute-start.31 = (f32[120,256]{1,0:T(8,128)S(1)}, f32[120,256]{1,0:T(8,128)S(1)}, u32[]{:S(2)}, u32[]{:S(2)}) collective-permute-start(f32[120,256]{1,0:T(8,128)S(1)} %collective-permute-done.30.refs_2_.refs_10_), channel_id=1, source_target_pairs={{0,8},{1,5},{2,10},{3,7},{8,16},{9,1},{10,18},{11,3},{16,24},{17,9... | collective-permute-start | bytes 368648 | tf_op jit(solution)/shard_map/ppermute | solution.py:332
  53.3 5.0 %collective-permute-start.38 = (f32[112,256]{1,0:T(8,128)S(1)}, f32[112,256]{1,0:T(8,128)S(1)}, u32[]{:S(2)}, u32[]{:S(2)}) collective-permute-start(f32[112,256]{1,0:T(8,128)S(1)} %collective-permute-done.37.refs_9_), channel_id=1, source_target_pairs={{0,8},{1,5},{2,10},{3,7},{8,16},{9,1},{10,18},{11,3},{16,24},{17,9... | collective-permute-start | bytes 344072 | tf_op jit(solution)/shard_map/ppermute | solution.py:332
  54.6 5.0 %collective-permute-start.32 = (f32[120,256]{1,0:T(8,128)S(1)}, f32[120,256]{1,0:T(8,128)S(1)}, u32[]{:S(2)}, u32[]{:S(2)}) collective-permute-start(f32[120,256]{1,0:T(8,128)S(1)} %collective-permute-done.31.refs_3_.refs_14_), channel_id=1, source_target_pairs={{0,8},{1,5},{2,10},{3,7},{8,16},{9,1},{10,18},{11,3},{16,24},{17,9... | collective-permute-start | bytes 368648 | tf_op jit(solution)/shard_map/ppermute | solution.py:332
  59.6 9.8 %collective-permute-start.33 = (f32[120,256]{1,0:T(8,128)S(1)}, f32[120,256]{1,0:T(8,128)S(1)}, u32[]{:S(2)}, u32[]{:S(2)}) collective-permute-start(f32[120,256]{1,0:T(8,128)S(1)} %collective-permute-done.32.refs_4_.refs_18_), channel_id=1, source_target_pairs={{0,8},{1,5},{2,10},{3,7},{8,16},{9,1},{10,18},{11,3},{16,24},{17,9... | collective-permute-start | bytes 368648 | tf_op jit(solution)/shard_map/ppermute | solution.py:332
  60.9 5.0 %collective-permute-start.56 = (f32[112,256]{1,0:T(8,128)S(1)}, f32[112,256]{1,0:T(8,128)S(1)}, u32[]{:S(2)}, u32[]{:S(2)}) collective-permute-start(f32[112,256]{1,0:T(8,128)S(1)} %collective-permute-done.55.refs_16_), channel_id=1, source_target_pairs={{0,8},{1,5},{2,10},{3,7},{8,16},{9,1},{10,18},{11,3},{16,24},{17,9... | collective-permute-start | bytes 344072 | tf_op jit(solution)/shard_map/ppermute | solution.py:332
  65.9 7.5 %collective-permute-start.57 = (f32[112,256]{1,0:T(8,128)S(1)}, f32[112,256]{1,0:T(8,128)S(1)}, u32[]{:S(2)}, u32[]{:S(2)}) collective-permute-start(f32[112,256]{1,0:T(8,128)S(1)} %collective-permute-done.56.refs_20_), channel_id=1, source_target_pairs={{0,8},{1,5},{2,10},{3,7},{8,16},{9,1},{10,18},{11,3},{16,24},{17,9... | collective-permute-start | bytes 344072 | tf_op jit(solution)/shard_map/ppermute | solution.py:332
  67.1 9.6 %collective-permute-start.50 = (f32[112,256]{1,0:T(8,128)S(1)}, f32[112,256]{1,0:T(8,128)S(1)}, u32[]{:S(2)}, u32[]{:S(2)}) collective-permute-start(f32[112,256]{1,0:T(8,128)S(1)} %collective-permute-done.49.refs_23_), channel_id=1, source_target_pairs={{0,8},{1,5},{2,10},{3,7},{8,16},{9,1},{10,18},{11,3},{16,24},{17,9... | collective-permute-start | bytes 344072 | tf_op jit(solution)/shard_map/ppermute | solution.py:332
  68.3 9.5 %collective-permute-start.41 = (f32[112,256]{1,0:T(8,128)S(1)}, f32[112,256]{1,0:T(8,128)S(1)}, u32[]{:S(2)}, u32[]{:S(2)}) collective-permute-start(f32[112,256]{1,0:T(8,128)S(1)} %collective-permute-done.40.refs_21_), channel_id=1, source_target_pairs={{0,8},{1,5},{2,10},{3,7},{8,16},{9,1},{10,18},{11,3},{16,24},{17,9... | collective-permute-start | bytes 344072 | tf_op jit(solution)/shard_map/ppermute | solution.py:332
  69.5 8.8 %collective-permute-start.43 = (f32[112,256]{1,0:T(8,128)S(1)}, f32[112,256]{1,0:T(8,128)S(1)}, u32[]{:S(2)}, u32[]{:S(2)}) collective-permute-start(f32[112,256]{1,0:T(8,128)S(1)} %unload.1), channel_id=1, source_target_pairs={{0,8},{1,5},{2,10},{3,7},{8,16},{9,1},{10,18},{11,3},{16,24},{17,9... | collective-permute-start | bytes 344072 | tf_op jit(solution)/shard_map/ppermute | solution.py:332
  73.4 5.8 %collective-permute-start.52 = (f32[112,256]{1,0:T(8,128)S(1)}, f32[112,256]{1,0:T(8,128)S(1)}, u32[]{:S(2)}, u32[]{:S(2)}) collective-permute-start(f32[112,256]{1,0:T(8,128)S(1)} %add.55.refs_3_), channel_id=1, source_target_pairs={{0,4},{1,9},{2,6},{3,11},{8,0},{9,17},{10,2},{11,19},{16,8},{17,25... | collective-permute-start | bytes 344072 | tf_op jit(solution)/shard_map/ppermute | solution.py:332
  76.7 7.7 %collective-permute-start.51 = (f32[112,256]{1,0:T(8,128)S(1)}, f32[112,256]{1,0:T(8,128)S(1)}, u32[]{:S(2)}, u32[]{:S(2)}) collective-permute-start(f32[112,256]{1,0:T(8,128)S(1)} %collective-permute-done.50.refs_27_), channel_id=1, source_target_pairs={{0,8},{1,5},{2,10},{3,7},{8,16},{9,1},{10,18},{11,3},{16,24},{17,9... | collective-permute-start | bytes 344072 | tf_op jit(solution)/shard_map/ppermute | solution.py:332
  77.8 6.5 %collective-permute-start.42 = (f32[112,256]{1,0:T(8,128)S(1)}, f32[112,256]{1,0:T(8,128)S(1)}, u32[]{:S(2)}, u32[]{:S(2)}) collective-permute-start(f32[112,256]{1,0:T(8,128)S(1)} %collective-permute-done.41.refs_25_), channel_id=1, source_target_pairs={{0,8},{1,5},{2,10},{3,7},{8,16},{9,1},{10,18},{11,3},{16,24},{17,9... | collective-permute-start | bytes 344072 | tf_op jit(solution)/shard_map/ppermute | solution.py:332
  78.3 6.1 %collective-permute-start.44 = (f32[112,256]{1,0:T(8,128)S(1)}, f32[112,256]{1,0:T(8,128)S(1)}, u32[]{:S(2)}, u32[]{:S(2)}) collective-permute-start(f32[112,256]{1,0:T(8,128)S(1)} %collective-permute-done.43.refs_26_), channel_id=1, source_target_pairs={{0,8},{1,5},{2,10},{3,7},{8,16},{9,1},{10,18},{11,3},{16,24},{17,9... | collective-permute-start | bytes 344072 | tf_op jit(solution)/shard_map/ppermute | solution.py:332
  (38 other events, 174.6 us)
